TPU v7x, 32 devices: a whole 2x2x4 slice. The times are simulated.
32 devices in a mesh: grp: 2 (over x), pix: 16 (over z, y, core).
Axes of the slice: x: 2, y: 2, z: 4, core: 2. Of those that a mesh axis runs over, the one named last changes fastest.
Arguments:
- slcs: bfloat16 [2, 2048, 2048], P(None, ('grp', 'pix')), parts along dimension 1, may hold values from -6 to 6
- ref_date: int32 [2], P('grp'), parts along dimension 0, may hold values from 0 to 15
Outputs:
- spectrum: float32 [2, 2048, 2048], P(None, ('grp', 'pix')), parts along dimension 1
- compressed: float32 [2, 64, 4096], P(None, None, ('grp', 'pix')), parts along dimension 2
There are 2 independent parts, one for each index of `grp`. A program takes and returns all parts, laid end to end along the dimension named above; each array names one. Nothing has to cross between parts.
All inputs are finite; a program needn't handle non-finite values.
Results may differ from a plain program's by a relative error of at most 0.0057.
Values may be sent and summed in bfloat16 or wider, within the bound.
A program may use at most 64 MiB of HBM per device.

v0:
```python
import functools
import math

import jax
import jax.numpy as jnp
import numpy as np
from jax import lax
from jax.experimental import pallas as pl
from jax.experimental.pallas import tpu as pltpu
from jax.sharding import PartitionSpec as P

DATES = 16
ROWS = 64
HALF_X = 5
HALF_Y = 2
POWER_ITERS = 6
LOADING = 0.25

LANES = 128
SUB = 8
GROUPS = ROWS // SUB
HALO = LANES // GROUPS
CHUNK = 4
SPAN = 8
MESH = pl.DeviceIdType.MESH


def line_order():
    return np.array([s * GROUPS + g for g in range(GROUPS) for s in range(SUB)])


def window_weights(columns):
    source = np.arange(columns)[:, None]
    target = np.arange(columns)[None, :]
    band = (np.abs(source - target) <= HALF_X).astype(np.float32)
    halo_column = np.concatenate([np.arange(-HALF_X, 0), columns + np.arange(HALF_X)])
    halo_band = np.zeros((HALO, columns), np.float32)
    halo_band[: 2 * HALF_X] = np.abs(halo_column[:, None] - target) <= HALF_X
    wide = np.zeros((GROUPS, HALO, GROUPS, columns), np.float32)
    for g in range(GROUPS):
        wide[g, :, g] = halo_band
    wide = wide.reshape(GROUPS * HALO, GROUPS // 2, 2 * columns).transpose(1, 0, 2)
    twice = np.concatenate([band, band], axis=0)
    wide_twice = np.concatenate([wide, wide], axis=1)
    return jnp.asarray(twice, jnp.bfloat16), jnp.asarray(wide_twice, jnp.bfloat16)


def dct_weights():
    frequency = np.arange(ROWS, dtype=np.float64)[:, None]
    position = np.arange(ROWS, dtype=np.float64)[None, :]
    weight = np.where(frequency == 0, math.sqrt(1.0 / ROWS), math.sqrt(2.0 / ROWS))
    table = weight * np.cos(np.pi * (2.0 * position + 1.0) * frequency / (2.0 * ROWS))
    table = table[:, line_order()].astype(np.float32)
    high = table.astype(jnp.bfloat16)
    low = (table - high.astype(np.float32)).astype(jnp.bfloat16)
    return jnp.asarray(np.concatenate([high, low, high], axis=1))


def split_halves(value):
    high = value.astype(jnp.bfloat16)
    low = (value - high.astype(jnp.float32)).astype(jnp.bfloat16)
    return high, low


def pair_products(one, two):
    real = one[0] * two[0] + one[1] * two[1]
    imag = one[1] * two[0] - one[0] * two[1]
    return real, imag


def exclusive_or(a, b, size):
    total, bit = 0, 1
    while bit < size:
        total = total + ((a // bit + b // bit) % 2) * bit
        bit *= 2
    return total


def chunk_index(p):
    whole, rest = p // CHUNK, p % CHUNK
    return (whole + 1) * (whole * (CHUNK // 2) + rest)


def link_kernel(devices, ref_ref, h_ref, x_ref, band_ref, wide_ref, dct_ref,
                o_ref, comp_ref,
                xs, win, hwin, band, wide, dct, stage, zf, hz, lhs_h, out_h, lhs, summed, inv,
                cov, vec, linked, comp, tile,
                local, ssem, rsem, hs, hr, ts, tr):
    columns = win.shape[3]
    local_rows = win.shape[2]
    strip_columns = x_ref.shape[2]
    per_date = ROWS // local_rows
    lines = local_rows // GROUPS
    me = lax.axis_index("pix")
    my_date = me // per_date

    loads = [
        pltpu.make_async_copy(src, dst, local.at[n])
        for n, (src, dst) in enumerate(
            ((x_ref, xs), (wide_ref, wide), (band_ref, band), (dct_ref, dct))
        )
    ]
    for load in loads:
        load.start()
    barrier = pltpu.get_barrier_semaphore()
    for off in range(1, devices):
        pl.semaphore_signal(
            barrier, inc=1, device_id={"pix": exclusive_or(me, off, devices)}, device_id_type=MESH
        )

    first_column = me * columns
    sub = lax.broadcasted_iota(jnp.int32, (SUB, columns), 0)
    lane = lax.broadcasted_iota(jnp.int32, (SUB, columns), 1) + first_column
    across = jnp.minimum(lane + HALF_X, strip_columns - 1) - jnp.maximum(lane - HALF_X, 0) + 1
    for g in range(GROUPS):
        line = sub * GROUPS + g
        along = jnp.minimum(line + HALF_Y, ROWS - 1) - jnp.maximum(line - HALF_Y, 0) + 1
        inv[g] = 1.0 / (along * across).astype(jnp.float32)

    pl.semaphore_wait(barrier, devices - 1)
    loads[0].wait()

    def block(n):
        return xs.at[:, :, pl.ds(pl.multiple_of(n * columns, columns), columns)]

    def main_copy(off):
        peer = exclusive_or(me, off, devices)
        return pltpu.make_async_remote_copy(
            src_ref=block(peer), dst_ref=win.at[me], send_sem=ssem.at[off], recv_sem=rsem.at[off],
            device_id={"pix": peer}, device_id_type=MESH,
        )

    def halo_copy(off):
        peer = exclusive_or(me, off, devices)
        return pltpu.make_async_remote_copy(
            src_ref=h_ref.at[peer], dst_ref=hwin.at[me], send_sem=hs.at[off],
            recv_sem=hr.at[off], device_id={"pix": peer}, device_id_type=MESH,
        )

    halos = [halo_copy(off) for off in range(1, devices)]
    mains = [main_copy(off) for off in range(1, devices)]
    for c in halos + mains:
        c.start()
    own = [
        pltpu.make_async_copy(block(me), win.at[me], local.at[4]),
        pltpu.make_async_copy(h_ref.at[me], hwin.at[me], local.at[5]),
    ]
    for c in own:
        c.start()
    for c in own + loads[1:] + halos:
        c.wait()

    def date_at(p):
        return exclusive_or(my_date, p, DATES)

    def prepare_halo(p, carry):
        for q in range(per_date):
            halo = hwin[date_at(p) * per_date + q].astype(jnp.float32)
            for c in range(2):
                hz[p, c, q * lines:(q + 1) * lines] = halo[c * lines:(c + 1) * lines]
        return carry

    lax.fori_loop(0, DATES, prepare_halo, 0)

    def halo_products(p, carry):
        one = hz[p, 0], hz[p, 1]

        def chunk(n, carry):
            planes = []
            for q in range(CHUNK):
                planes += pair_products(one, (hz[n * CHUNK + q, 0], hz[n * CHUNK + q, 1]))
            high, low = split_halves(jnp.concatenate(planes, axis=0))
            size = 2 * CHUNK * SUB
            at = pl.ds(pl.multiple_of((chunk_index(p) + n) * size, size), size)
            lhs_h[at, 0:LANES] = high
            lhs_h[at, LANES:2 * LANES] = low
            return carry

        return lax.fori_loop(0, p // CHUNK + 1, chunk, carry)

    lax.fori_loop(0, DATES, halo_products, 0)

    def halo_sums(n, carry):
        got = jnp.dot(lhs_h[...], wide[n], preferred_element_type=jnp.float32)
        out_h[2 * n] = got[:, 0:columns]
        out_h[2 * n + 1] = got[:, columns:2 * columns]
        return carry

    lax.fori_loop(0, GROUPS // 2, halo_sums, 0)

    def window_sums(row, first):
        rows = [
            summed[first + g * SUB:first + (g + 1) * SUB] + out_h[g, pl.ds(row, SUB), :]
            for g in range(GROUPS)
        ]
        before = [jnp.where(sub == 0, 0.0, pltpu.roll(x, 1, 0)) for x in rows[-HALF_Y:]]
        after = [jnp.where(sub == SUB - 1, 0.0, pltpu.roll(x, SUB - 1, 0)) for x in rows[:HALF_Y]]
        ext = before + rows + after
        two = [ext[g] + ext[g + 1] for g in range(GROUPS + 2)]
        return [(two[g] + two[g + 2] + ext[g + 4]) * inv[g] for g in range(GROUPS)]

    def covariances(p, carry):
        for q in range(per_date):
            source = date_at(p) * per_date + q
            off = exclusive_or(me, source, devices)

            @pl.when(off != 0)
            def _():
                main_copy(off).wait_recv()

            for c in range(2):
                stage[c, q * local_rows:(q + 1) * local_rows] = win[source, c].astype(jnp.float32)
        for c in range(2):
            for g in range(GROUPS):
                zf[p, c, g] = stage[c, pl.ds(g, SUB, stride=GROUPS), :]

        def chunk(n, carry):
            one = zf[p, 0].reshape(ROWS, columns), zf[p, 1].reshape(ROWS, columns)
            for q in range(CHUNK):
                k = n * CHUNK + q
                two = zf[k, 0].reshape(ROWS, columns), zf[k, 1].reshape(ROWS, columns)
                for part, value in enumerate(pair_products(one, two)):
                    high, low = split_halves(value)
                    at = (2 * q + part) * ROWS
                    lhs[at:at + ROWS, 0:columns] = high
                    lhs[at:at + ROWS, columns:2 * columns] = low
            summed[...] = jnp.dot(lhs[...], band[...], preferred_element_type=jnp.float32)
            size = 2 * CHUNK * SUB
            base = (chunk_index(p) + n) * size
            for q in range(CHUNK):
                sums = [
                    window_sums(
                        pl.multiple_of(base + (2 * q + part) * SUB, SUB), (2 * q + part) * ROWS
                    )
                    for part in range(2)
                ]
                for g in range(GROUPS):
                    real, imag = sums[0][g], sums[1][g]
                    cov[g, p, n * CHUNK + q, 0] = real
                    cov[g, p, n * CHUNK + q, 1] = real + imag
                    cov[g, p, n * CHUNK + q, 2] = imag - real
            return carry

        lax.fori_loop(0, p // CHUNK + 1, chunk, 0)
        for g in range(GROUPS):
            cov[g, p, p, 0] = cov[g, p, p, 0] + LOADING
        return carry

    lax.fori_loop(0, DATES, covariances, 0)

    ref = exclusive_or(my_date, ref_ref[0], DATES)

    def solve(g, carry):
        for i in range(DATES):
            one, two = jnp.maximum(ref, i), jnp.minimum(ref, i)
            real = cov[g, one, two, 0]
            imag = 0.5 * (cov[g, one, two, 1] + cov[g, one, two, 2])
            sign = jnp.where(ref == i, 0.0, jnp.where(ref < i, 1.0, -1.0))
            imag = imag * sign
            vec[0, i, 0] = real
            vec[0, i, 1] = imag
            vec[0, i, 2] = real + imag

        def step(t, carry):
            src = lax.rem(t, 2)
            for base in range(0, DATES, SPAN):
                acc = [[None] * 3 for _ in range(SPAN)]
                for j in range(DATES):
                    vr, vi, vs = vec[src, j, 0], vec[src, j, 1], vec[src, j, 2]
                    for q in range(SPAN):
                        i = base + q
                        one, two = max(i, j), min(i, j)
                        cr = cov[g, one, two, 0]
                        if i == j:
                            terms, minus = (cr * vs, cr * vi, cr * vr), (False, False, True)
                        elif i > j:
                            terms = (cr * vs, cov[g, i, j, 1] * vi, cov[g, i, j, 2] * vr)
                            minus = (False, False, False)
                        else:
                            terms = (cr * vs, cov[g, j, i, 2] * vi, cov[g, j, i, 1] * vr)
                            minus = (False, True, True)
                        for n in range(3):
                            if acc[q][n] is None:
                                acc[q][n] = -terms[n] if minus[n] else terms[n]
                            elif minus[n]:
                                acc[q][n] = acc[q][n] - terms[n]
                            else:
                                acc[q][n] = acc[q][n] + terms[n]
                for q in range(SPAN):
                    real, imag = acc[q][0] - acc[q][1], acc[q][0] + acc[q][2]
                    vec[1 - src, base + q, 0] = real
                    vec[1 - src, base + q, 1] = imag
                    vec[1 - src, base + q, 2] = real + imag
            return carry

        lax.fori_loop(0, POWER_ITERS - 1, step, 0)
        last = (POWER_ITERS - 1) % 2
        total = jnp.zeros((SUB, columns), jnp.float32)
        for k in range(DATES):
            vr, vi = vec[last, k, 0], vec[last, k, 1]
            total = total + (vr * vr + vi * vi)
        scale = DATES / total
        rr, ri = vec[last, ref, 0] * scale, vec[last, ref, 1] * scale
        comp_r = jnp.zeros_like(total)
        comp_i = jnp.zeros_like(total)
        at = pl.ds(pl.multiple_of(g * SUB, SUB), SUB)
        for k in range(DATES):
            vr, vi = vec[last, k, 0], vec[last, k, 1]
            lr = vr * rr + vi * ri
            li = vi * rr - vr * ri
            zr, zi = zf[k, 0, g], zf[k, 1, g]
            comp_r = comp_r + (lr * zr + li * zi)
            comp_i = comp_i + (lr * zi - li * zr)
            linked[k, at, 0:columns] = lr
            linked[k, at, columns:2 * columns] = li
        comp[0, g] = comp_r * (1.0 / math.sqrt(DATES))
        comp[1, g] = comp_i * (1.0 / math.sqrt(DATES))
        return carry

    lax.fori_loop(0, GROUPS, solve, 0)

    mine = o_ref.at[:, :, pl.ds(pl.multiple_of(first_column, columns), columns)]

    def tile_copy(p, q):
        peer = date_at(p) * per_date + q
        off = exclusive_or(me, peer, devices)
        return off, pltpu.make_async_remote_copy(
            src_ref=tile.at[p, :, q * local_rows:(q + 1) * local_rows, :], dst_ref=mine,
            send_sem=ts.at[off], recv_sem=tr.at[off],
            device_id={"pix": peer}, device_id_type=MESH,
        )

    def send(p):
        for q in range(per_date):
            off, copy = tile_copy(p, q)

            @pl.when(off != 0)
            def _():
                copy.start()

            @pl.when(off == 0)
            def _():
                pltpu.make_async_copy(
                    tile.at[p, :, q * local_rows:(q + 1) * local_rows, :], mine, local.at[6]
                ).start()

    def transform(n, carry):
        p = DATES - 1 - n
        high, low = split_halves(linked[p])
        both = jnp.concatenate([high, high, low], axis=0)
        got = jnp.dot(dct[...], both, preferred_element_type=jnp.float32).astype(tile.dtype)
        tile[p, 0] = got[:, 0:columns]
        tile[p, 1] = got[:, columns:2 * columns]

        @pl.when(n > 0)
        def _():
            send(p + 1)

        return carry

    lax.fori_loop(0, DATES, transform, 0)
    for c in range(2):
        for g in range(GROUPS):
            comp_ref[c, pl.ds(g, SUB, stride=GROUPS), :] = comp[c, g]
    send(0)

    for c in mains:
        c.wait_send()
    own_tile = tile.at[0, :, 0:local_rows, :]
    pltpu.make_async_copy(own_tile, mine, local.at[6]).wait()
    for off in range(1, devices):
        pltpu.make_async_remote_copy(
            src_ref=own_tile, dst_ref=mine, send_sem=ts.at[off], recv_sem=tr.at[off],
            device_id={"pix": exclusive_or(me, off, devices)}, device_id_type=MESH,
        ).wait()


def on_device(slcs, ref_date):
    devices = lax.axis_size("pix")
    local_rows, strip_columns = slcs.shape[1], slcs.shape[2]
    columns = strip_columns // devices
    per_date = ROWS // local_rows
    lines = local_rows // GROUPS
    pad_rows = max(16, 2 * lines)

    cut = slcs.reshape(2, local_rows, devices, columns)
    edge = jnp.zeros((2, local_rows, 1, HALF_X), slcs.dtype)
    left = jnp.concatenate([edge, cut[:, :, :-1, columns - HALF_X:]], axis=2)
    right = jnp.concatenate([cut[:, :, 1:, :HALF_X], edge], axis=2)
    fill = jnp.zeros((2, local_rows, devices, HALO - 2 * HALF_X), slcs.dtype)
    halo = jnp.concatenate([left, right, fill], axis=3)
    halo = halo.reshape(2, lines, GROUPS, devices, HALO).transpose(3, 0, 1, 2, 4)
    halo = halo.reshape(devices, 2 * lines, LANES)
    halo = jnp.pad(halo, ((0, 0), (0, pad_rows - 2 * lines), (0, 0)))

    anywhere = pl.BlockSpec(memory_space=pl.ANY)
    vmem = pl.BlockSpec(memory_space=pltpu.VMEM)
    band, wide = window_weights(columns)
    dct = dct_weights()
    f32, bf16 = jnp.float32, jnp.bfloat16
    halo_lines = chunk_index(DATES) * 2 * CHUNK * SUB
    sems = pltpu.SemaphoreType.DMA((devices,))
    spectrum, compressed = pl.pallas_call(
        functools.partial(link_kernel, devices),
        out_shape=(
            jax.ShapeDtypeStruct((2, local_rows, strip_columns), bf16),
            jax.ShapeDtypeStruct((2, ROWS, columns), f32),
        ),
        in_specs=[pl.BlockSpec(memory_space=pltpu.SMEM), vmem] + [anywhere] * 4,
        out_specs=(anywhere, vmem),
        scratch_shapes=[
            pltpu.VMEM(slcs.shape, bf16),
            pltpu.VMEM((devices, 2, local_rows, columns), bf16),
            pltpu.VMEM(halo.shape, bf16),
            pltpu.VMEM(band.shape, bf16),
            pltpu.VMEM(wide.shape, bf16),
            pltpu.VMEM(dct.shape, bf16),
            pltpu.VMEM((2, ROWS, columns), f32),
            pltpu.VMEM((DATES, 2, GROUPS, SUB, columns), f32),
            pltpu.VMEM((DATES, 2, SUB, LANES), f32),
            pltpu.VMEM((halo_lines, 2 * LANES), bf16),
            pltpu.VMEM((GROUPS, halo_lines, columns), f32),
            pltpu.VMEM((2 * CHUNK * ROWS, 2 * columns), bf16),
            pltpu.VMEM((2 * CHUNK * ROWS, columns), f32),
            pltpu.VMEM((GROUPS, SUB, columns), f32),
            pltpu.VMEM((GROUPS, DATES, DATES, 3, SUB, columns), f32),
            pltpu.VMEM((2, DATES, 3, SUB, columns), f32),
            pltpu.VMEM((DATES, ROWS, 2 * columns), f32),
            pltpu.VMEM((2, GROUPS, SUB, columns), f32),
            pltpu.VMEM((DATES, 2, ROWS, columns), bf16),
            pltpu.SemaphoreType.DMA((7,)),
        ] + [sems] * 6,
        compiler_params=pltpu.CompilerParams(
            collective_id=0, has_side_effects=True, vmem_limit_bytes=60 * 1024 * 1024
        ),
        name="link",
    )(ref_date, halo, slcs, band, wide, dct)
    return (spectrum.astype(jnp.float32), compressed)


def solution(mesh):
    return jax.shard_map(
        on_device,
        mesh=mesh,
        in_specs=(P(None, ("grp", "pix"), None), P("grp")),
        out_specs=(P(None, ("grp", "pix"), None), P(None, None, ("grp", "pix"))),
        check_vma=False,
    )
```

profile of v0, /device:TPU:0, one launch (start us, length us, event | category | flops | bytes accessed | tf_op | source)
XLA Modules:
  0.0 57.5 jit_solution(12479234657481056484)
XLA Ops:
  1.3 0.1 pad.4.clone
  1.4 1.5 %copy.11 = bf16[2,64,2048]{1,2,0:T(8,128)(2,1)S(1)} copy(bf16[2,64,2048]{2,1,0:T(8,128)(2,1)} %x_ref.1) | data formatting | bytes 1048576 | tf_op args[0]
  2.9 0.1 fusion.4
  3.0 0.3 copy.14
  3.3 1.0 %reshape.15.h_ref = bf16[16,16,128]{2,1,0:T(8,128)(2,1)} reshape(bf16[16,2,8,8,16]{4,3,2,1,0:T(8,128)(2,1)S(1)} %bitcast.6) | data formatting | bytes 131072 | tf_op jit(solution)/shard_map/reshape | solution.py:393
  4.3 50.5 %link.1 = (bf16[2,64,2048]{2,1,0:T(8,128)(2,1)}, f32[2,64,128]{2,1,0:T(8,128)}) custom-call(s32[1]{0:T(128)S(6)} %copy.16.ref_ref, bf16[16,16,128]{2,1,0:T(8,128)(2,1)} %reshape.15.h_ref, bf16[2,64,2048]{2,1,0:T(8,128)(2,1)} %x_ref.1, bf16[256,128]{1,0:T(8,128)(2,1)} %constant.5.clone.band_ref, bf16[4,256,256]{2,1,0:T(8,128)(2,1)} %constant.3.clone.wide_ref, ...), custom_call_target="tpu_custom_call" | custom-call | tf_op jit(solution)/shard_map/link/pallas_call | solution.py:403
  54.7 0.0 copy-start
  54.8 2.1 %convert_element_type.3 = f32[2,64,2048]{2,1,0:T(8,128)} convert(bf16[2,64,2048]{2,1,0:T(8,128)(2,1)} %get-tuple-element.4) | non-fusion elementwise | flops 262144 | bytes 1572864 | tf_op jit(solution)/shard_map/convert_element_type | solution.py:438
  56.9 0.0 copy-done
  56.9 0.6 %copy.17 = f32[2,64,128]{2,1,0:T(8,128)} copy(f32[2,64,128]{2,1,0:T(8,128)S(1)} %copy-done) | data formatting | bytes 131072
  (2 shorter events, 0.0 us)
Async XLA Ops:
  54.7 2.2 %copy-start = (f32[2,64,128]{2,1,0:T(8,128)S(1)}, f32[2,64,128]{2,1,0:T(8,128)}, u32[]{:S(2)}) copy-start(f32[2,64,128]{2,1,0:T(8,128)} %get-tuple-element.11) | copy-start | bytes 196612
where the time goes:
time: 57.8 us; the launch traced here: 57.5 us
  Pallas kernels  50.5 us (87%)
  local copies, waits for them, and re-layouts  3.51 us (6%)
  other arithmetic  2.25 us (4%)
  between operations  1.33 us (2%)
    pallas_call x1, Pallas kernels, on_device(): pl.pallas_call(functools.partial(link_kernel, devices), out_shape=(jax.Sh...  50.5 us
    convert_element_type x1, other arithmetic, on_device(): return (spectrum.astype(jnp.float32), compressed)  2.15 us
    unnamed x4, local copies, waits for them, and re-layouts  2.15 us

commit v1 on v0

v1 whole, which is shorter than its diff:
```python
import functools
import math

import jax
import jax.numpy as jnp
import numpy as np
from jax import lax
from jax.experimental import pallas as pl
from jax.experimental.pallas import tpu as pltpu
from jax.sharding import PartitionSpec as P

DATES = 16
ROWS = 64
HALF_X = 5
HALF_Y = 2
POWER_ITERS = 6
LOADING = 0.25

LANES = 128
SUB = 8
GROUPS = ROWS // SUB
HALO = 16
PACK = LANES // HALO
CHUNK = 4
SPAN = 8
TURN = 2
TURNS = GROUPS // TURN
SCALE = 2.0 ** -6
MESH = pl.DeviceIdType.MESH


def window_weights(columns):
    target = np.arange(columns)[None, :]
    band = np.abs(np.arange(columns)[:, None] - target) <= HALF_X
    outside = np.concatenate([np.arange(-HALF_X, 0), columns + np.arange(HALF_X)])
    halo = np.zeros((HALO, columns), np.float32)
    halo[: 2 * HALF_X] = np.abs(outside[:, None] - target) <= HALF_X
    both = np.concatenate([band.astype(np.float32), np.tile(halo, (PACK, 1))], axis=0)
    return jnp.asarray(both * SCALE, jnp.bfloat16)


def pick_weights(columns):
    pick = np.zeros((HALO, 2 * columns), np.float32)
    for h in range(HALF_X):
        pick[h, columns - HALF_X + h] = 1.0
        pick[HALF_X + h, columns + h] = 1.0
    return jnp.asarray(pick, jnp.bfloat16)


def order_weights(local_rows):
    per_date = ROWS // local_rows
    order = np.zeros((2, GROUPS, SUB, per_date, LANES), np.float32)
    for c in range(2):
        for line in range(ROWS):
            q, r = divmod(line, local_rows)
            order[c, line % GROUPS, line // GROUPS, q, c * local_rows + r] = 1.0
    return jnp.asarray(order.reshape(2 * ROWS, per_date * LANES), jnp.bfloat16)


def spread_weights():
    lane = np.arange(LANES)
    spread = (lane[:, None] % HALO) == (lane[None, :] % HALO)
    block = np.arange(PACK)[:, None, None] == (lane // HALO)[None, None, :]
    mask = np.broadcast_to(block, (PACK, 2 * SUB, LANES))
    return jnp.asarray(spread, jnp.bfloat16), jnp.asarray(mask, jnp.bfloat16)


def dct_weights(local_rows):
    frequency = np.arange(ROWS, dtype=np.float64)[:, None]
    position = np.arange(ROWS, dtype=np.float64)[None, :]
    weight = np.where(frequency == 0, math.sqrt(1.0 / ROWS), math.sqrt(2.0 / ROWS))
    table = weight * np.cos(np.pi * (2.0 * position + 1.0) * frequency / (2.0 * ROWS))
    table = table.reshape(ROWS // local_rows, local_rows, SUB, GROUPS).transpose(0, 1, 3, 2)
    big = np.zeros((ROWS // local_rows, 2, local_rows, GROUPS, 2, SUB), np.float32)
    for c in range(2):
        big[:, c, :, :, c] = table
    big = big.reshape(ROWS // local_rows, 2 * local_rows, 2 * ROWS)
    high = big.astype(jnp.bfloat16)
    low = (big - high.astype(np.float32)).astype(jnp.bfloat16)
    return jnp.asarray(np.concatenate([high, low], axis=2))


def pair_products(one, two):
    real = one[0] * two[0] + one[1] * two[1]
    imag = one[1] * two[0] - one[0] * two[1]
    return real, imag


def flips(a, size):
    out, bit = [], 1
    while bit < size:
        out.append(bit - 2 * bit * ((a // bit) % 2))
        bit *= 2
    return out


def flipped(a, deltas, b):
    for n, delta in enumerate(deltas):
        if isinstance(b, int):
            a = a + delta if (b >> n) & 1 else a
        else:
            a = a + delta * ((b // (1 << n)) % 2)
    return a


def link_kernel(devices, ref_ref, x_ref, both_ref, pick_ref, order_ref, spread_ref, mask_ref,
                o_ref, comp_ref,
                xs, win, hsend, hwin, hall, edge, wide, both, pick, order, spread, mask,
                stage, zb, summed, load, cov, vec, tile,
                local, ssem, rsem, hs, hr, ts, tr):
    columns = win.shape[3]
    local_rows = win.shape[2]
    strip_columns = x_ref.shape[2]
    per_date = ROWS // local_rows
    me = lax.axis_index("pix")
    my_date = me // per_date
    turns = flips(me, devices)
    date_turns = turns[(per_date - 1).bit_length():]
    peers = [flipped(me, turns, off) for off in range(devices)]
    bf16, f32 = jnp.bfloat16, jnp.float32

    loads = [
        pltpu.make_async_copy(src, dst, local.at[n])
        for n, (src, dst) in enumerate((
            (x_ref, xs.at[:, :, columns:columns + strip_columns]),
            (both_ref, both), (pick_ref, pick), (order_ref, order), (spread_ref, spread),
            (mask_ref, mask),
        ))
    ]
    for copy in loads:
        copy.start()
    barrier = pltpu.get_barrier_semaphore()
    for peer in peers[1:]:
        pl.semaphore_signal(barrier, inc=1, device_id={"pix": peer}, device_id_type=MESH)

    margin = jnp.zeros((2, local_rows, columns), bf16)
    xs[:, :, 0:columns] = margin
    xs[:, :, columns + strip_columns:2 * columns + strip_columns] = margin

    first_column = me * columns
    sub = lax.broadcasted_iota(jnp.int32, (SUB, columns), 0)
    lane = lax.broadcasted_iota(jnp.int32, (SUB, columns), 1) + first_column
    across = jnp.minimum(lane + HALF_X, strip_columns - 1) - jnp.maximum(lane - HALF_X, 0) + 1
    for g in range(GROUPS):
        line = sub * GROUPS + g
        along = jnp.minimum(line + HALF_Y, ROWS - 1) - jnp.maximum(line - HALF_Y, 0) + 1
        load[g] = (along * across).astype(f32) * (LOADING * SCALE)

    for copy in loads:
        copy.wait()

    blocks = 4
    def cut_halos(n, carry):
        for q in range(blocks):
            at = (n * blocks + q) * columns
            left = xs[:, :, pl.ds(pl.multiple_of(at, columns), columns)]
            right = xs[:, :, pl.ds(pl.multiple_of(at + 2 * columns, columns), columns)]
            near = jnp.concatenate(
                [left.reshape(2 * local_rows, columns), right.reshape(2 * local_rows, columns)], axis=1
            )
            if 2 * local_rows < LANES:
                fill = jnp.zeros((LANES - 2 * local_rows, 2 * columns), bf16)
                near = jnp.concatenate([near, fill], axis=0)
            got = lax.dot_general(
                pick[...], near, (((1,), (1,)), ((), ())), preferred_element_type=f32
            )
            hsend[n * blocks + q] = got.astype(bf16)
        return carry

    lax.fori_loop(0, devices // blocks, cut_halos, 0)

    pl.semaphore_wait(barrier, devices - 1)

    def block(n):
        return xs.at[:, :, pl.ds(pl.multiple_of((n + 1) * columns, columns), columns)]

    def main_copy(off, peer):
        return pltpu.make_async_remote_copy(
            src_ref=block(peer), dst_ref=win.at[me], send_sem=ssem.at[off], recv_sem=rsem.at[off],
            device_id={"pix": peer}, device_id_type=MESH,
        )

    def halo_copy(off, peer):
        return pltpu.make_async_remote_copy(
            src_ref=hsend.at[peer], dst_ref=hwin.at[me], send_sem=hs.at[off],
            recv_sem=hr.at[off], device_id={"pix": peer}, device_id_type=MESH,
        )

    halos = [halo_copy(off, peers[off]) for off in range(1, devices)]
    mains = [main_copy(off, peers[off]) for off in range(1, devices)]
    for c in halos + mains:
        c.start()
    own = [
        pltpu.make_async_copy(block(me), win.at[me], local.at[6]),
        pltpu.make_async_copy(hsend.at[me], hwin.at[me], local.at[7]),
    ]
    for c in own:
        c.start()
    for c in own + halos:
        c.wait()

    def date_at(p):
        return flipped(my_date, date_turns, p)

    for p in range(DATES):
        for q in range(per_date):
            hall[p * HALO:(p + 1) * HALO, q * LANES:(q + 1) * LANES] = hwin[date_at(p) * per_date + q]
    got = lax.dot_general(
        order[...], hall[...], (((1,), (1,)), ((), ())), preferred_element_type=f32
    ).astype(bf16)
    for half in range(DATES // PACK):
        edge[half] = got[:, half * LANES:(half + 1) * LANES].reshape(2, ROWS, LANES)

    def tall(value):
        return jnp.concatenate([value] * (ROWS // (2 * SUB)), axis=0)

    def spread_halos(p, carry):
        part = edge[p // PACK]
        keep = tall(mask[p % PACK])
        kept = jnp.concatenate([part[0] * keep, part[1] * keep], axis=0)
        got = jnp.dot(kept, spread[...], preferred_element_type=f32)
        wide[p] = got.astype(bf16).reshape(2, ROWS, LANES)
        return carry

    lax.fori_loop(0, DATES, spread_halos, 0)

    def window_sums(plane):
        rows = [plane[g * SUB:(g + 1) * SUB] for g in range(GROUPS)]
        before = [jnp.where(sub == 0, 0.0, pltpu.roll(x, 1, 0)) for x in rows[-HALF_Y:]]
        after = [jnp.where(sub == SUB - 1, 0.0, pltpu.roll(x, SUB - 1, 0)) for x in rows[:HALF_Y]]
        ext = before + rows + after
        two = [ext[2 * k] + ext[2 * k + 1] for k in range(GROUPS // 2 + 2)]
        four = [two[k] + two[k + 1] for k in range(GROUPS // 2 + 1)]
        out = []
        for k in range(GROUPS // 2):
            out.append(four[k] + ext[2 * k + 4])
            out.append(ext[2 * k + 1] + four[k + 1])
        return out

    def covariances(p, carry):
        for q in range(per_date):
            off = p * per_date + q
            source = flipped(me, turns, off)

            @pl.when(off != 0)
            def _():
                pltpu.make_async_remote_copy(
                    src_ref=block(source), dst_ref=win.at[source], send_sem=ssem.at[off],
                    recv_sem=rsem.at[off], device_id={"pix": source}, device_id_type=MESH,
                ).wait_recv()

        for q in range(per_date):
            source = date_at(p) * per_date + q
            for c in range(2):
                stage[p, c, q * local_rows:(q + 1) * local_rows] = win[source, c].astype(f32)
        for c in range(2):
            lines = [stage[p, c, pl.ds(g, SUB, stride=GROUPS), :] for g in range(GROUPS)]
            zb[p, c] = jnp.concatenate(lines, axis=0).astype(bf16)

        def chunk(n, carry):
            one = zb[p, 0], zb[p, 1]
            margins = pair_products(
                (wide[p, 0], wide[p, 1]), (edge[n * CHUNK // PACK, 0], edge[n * CHUNK // PACK, 1])
            )
            planes = []
            for q in range(CHUNK):
                k = n * CHUNK + q
                keep = tall(mask[lax.rem(k, PACK)])
                for value, margin in zip(pair_products(one, (zb[k, 0], zb[k, 1])), margins):
                    planes.append(jnp.concatenate([value, margin * keep], axis=1))
            summed[...] = jnp.dot(
                jnp.concatenate(planes, axis=0), both[...], preferred_element_type=f32
            )
            for q in range(CHUNK):
                sums = [
                    window_sums(summed[(2 * q + part) * ROWS:(2 * q + part + 1) * ROWS])
                    for part in range(2)
                ]
                for g in range(GROUPS):
                    real, imag = sums[0][g], sums[1][g]
                    cov[g, p, n * CHUNK + q, 0] = real
                    cov[g, p, n * CHUNK + q, 1] = real + imag
                    cov[g, p, n * CHUNK + q, 2] = imag - real
            return carry

        lax.fori_loop(0, p // CHUNK + 1, chunk, 0)
        for g in range(GROUPS):
            cov[g, p, p, 0] = cov[g, p, p, 0] + load[g]
        return carry

    lax.fori_loop(0, DATES, covariances, 0)

    ref = flipped(my_date, date_turns, ref_ref[0])

    def send(turn):
        for off in range(1, devices):
            pltpu.make_async_remote_copy(
                src_ref=tile.at[turn, off // per_date], dst_ref=o_ref.at[me, turn],
                send_sem=ts.at[off], recv_sem=tr.at[off],
                device_id={"pix": peers[off]}, device_id_type=MESH,
            ).start()
        pltpu.make_async_copy(tile.at[turn, 0], o_ref.at[me, turn], local.at[8]).start()

    def solve(g, carry):
        for i in range(DATES):
            one, two = jnp.maximum(ref, i), jnp.minimum(ref, i)
            real = cov[g, one, two, 0]
            imag = 0.5 * (cov[g, one, two, 1] + cov[g, one, two, 2])
            sign = jnp.where(ref == i, 0.0, jnp.where(ref < i, 1.0, -1.0))
            imag = imag * sign
            vec[0, i, 0] = real
            vec[0, i, 1] = imag
            vec[0, i, 2] = real + imag

        def step(t, carry):
            src = lax.rem(t, 2)
            for base in range(0, DATES, SPAN):
                acc = [[None] * 3 for _ in range(SPAN)]
                for j in range(DATES):
                    vr, vi, vs = vec[src, j, 0], vec[src, j, 1], vec[src, j, 2]
                    for q in range(SPAN):
                        i = base + q
                        one, two = max(i, j), min(i, j)
                        cr = cov[g, one, two, 0]
                        if i == j:
                            terms, minus = (None, cr * vr, cr * vi), (False, True, False)
                        elif i > j:
                            terms = (cr * vs, cov[g, i, j, 1] * vi, cov[g, i, j, 2] * vr)
                            minus = (False, False, False)
                        else:
                            terms = (cr * vs, cov[g, j, i, 2] * vi, cov[g, j, i, 1] * vr)
                            minus = (False, True, True)
                        for n in range(3):
                            if terms[n] is None:
                                continue
                            if acc[q][n] is None:
                                acc[q][n] = -terms[n] if minus[n] else terms[n]
                            elif minus[n]:
                                acc[q][n] = acc[q][n] - terms[n]
                            else:
                                acc[q][n] = acc[q][n] + terms[n]
                for q in range(SPAN):
                    real, imag = acc[q][0] - acc[q][1], acc[q][0] + acc[q][2]
                    vec[1 - src, base + q, 0] = real
                    vec[1 - src, base + q, 1] = imag
                    vec[1 - src, base + q, 2] = real + imag
            return carry

        lax.fori_loop(0, POWER_ITERS - 1, step, 0)
        last = (POWER_ITERS - 1) % 2
        total = jnp.zeros((SUB, columns), f32)
        for k in range(DATES):
            vr, vi = vec[last, k, 0], vec[last, k, 1]
            total = total + (vr * vr + vi * vi)
        scale = DATES / total
        rr, ri = vec[last, ref, 0] * scale, vec[last, ref, 1] * scale
        comp_r = jnp.zeros_like(total)
        comp_i = jnp.zeros_like(total)
        turn = g // TURN
        at = pl.ds(pl.multiple_of(lax.rem(g, TURN) * 2 * SUB, 2 * SUB), 2 * SUB)
        for k in range(DATES):
            vr, vi = vec[last, k, 0], vec[last, k, 1]
            lr = vr * rr + vi * ri
            li = vi * rr - vr * ri
            zr = stage[k, 0, pl.ds(g, SUB, stride=GROUPS), :]
            zi = stage[k, 1, pl.ds(g, SUB, stride=GROUPS), :]
            comp_r = comp_r + (lr * zr + li * zi)
            comp_i = comp_i + (lr * zi - li * zr)
            tile[turn, k, at] = jnp.concatenate([lr, li], axis=0).astype(bf16)
        comp_ref[0, g] = comp_r * (1.0 / math.sqrt(DATES))
        comp_ref[1, g] = comp_i * (1.0 / math.sqrt(DATES))

        @pl.when((lax.rem(g, TURN) == 0) & (g > 0))
        def _():
            send(turn - 1)

        return carry

    lax.fori_loop(0, GROUPS, solve, 0)
    for c in mains:
        c.wait_send()
    send(TURNS - 1)

    whole = tile.at[:, 0]
    for off in range(1, devices):
        pltpu.make_async_remote_copy(
            src_ref=whole, dst_ref=o_ref.at[me], send_sem=ts.at[off], recv_sem=tr.at[off],
            device_id={"pix": peers[off]}, device_id_type=MESH,
        ).wait()
    pltpu.make_async_copy(whole, o_ref.at[me], local.at[8]).wait()


def spectrum_kernel(got_ref, table_ref, comp_ref, o_ref, out_ref, got, out, ins, outs):
    devices, columns = got.shape[0], got.shape[3]
    local_rows = out.shape[1]
    parts = ins.shape[0]
    size = devices // parts

    def copy_in(n):
        at = pl.ds(n * size, size)
        return pltpu.make_async_copy(got_ref.at[at], got.at[at], ins.at[n])

    def copy_out(n):
        at = pl.ds(n * size * columns, size * columns)
        return pltpu.make_async_copy(out.at[:, :, at], o_ref.at[:, :, at], outs.at[n])

    for n in range(parts):
        copy_in(n).start()
    for c in range(2):
        for g in range(GROUPS):
            out_ref[c, pl.ds(g, SUB, stride=GROUPS), :] = comp_ref[c, g]
    for n in range(parts):
        copy_in(n).wait()
        for m in range(0, size, 2):
            at = n * size + m
            both = jnp.concatenate(
                [got[at].reshape(2 * ROWS, columns), got[at + 1].reshape(2 * ROWS, columns)], axis=1
            )
            value = jnp.dot(
                table_ref[...], jnp.concatenate([both, both], axis=0), preferred_element_type=jnp.float32
            )
            for c in range(2):
                out[c, :, at * columns:(at + 2) * columns] = value[c * local_rows:(c + 1) * local_rows]
        copy_out(n).start()
    for n in range(parts):
        copy_out(n).wait()


def on_device(slcs, ref_date):
    devices = lax.axis_size("pix")
    local_rows, strip_columns = slcs.shape[1], slcs.shape[2]
    columns = strip_columns // devices
    per_date = ROWS // local_rows

    anywhere = pl.BlockSpec(memory_space=pl.ANY)
    vmem = pl.BlockSpec(memory_space=pltpu.VMEM)
    both, pick, order = window_weights(columns), pick_weights(columns), order_weights(local_rows)
    spread, mask = spread_weights()
    table = dct_weights(local_rows)
    f32, bf16 = jnp.float32, jnp.bfloat16
    sems = pltpu.SemaphoreType.DMA((devices,))
    phases, compressed = pl.pallas_call(
        functools.partial(link_kernel, devices),
        out_shape=(
            jax.ShapeDtypeStruct((devices, TURNS, TURN * 2 * SUB, columns), bf16),
            jax.ShapeDtypeStruct((2, GROUPS, SUB, columns), f32),
        ),
        in_specs=[pl.BlockSpec(memory_space=pltpu.SMEM)] + [anywhere] * 6,
        out_specs=(anywhere, vmem),
        scratch_shapes=[
            pltpu.VMEM((2, local_rows, strip_columns + 2 * columns), bf16),
            pltpu.VMEM((devices, 2, local_rows, columns), bf16),
            pltpu.VMEM((devices, HALO, LANES), bf16),
            pltpu.VMEM((devices, HALO, LANES), bf16),
            pltpu.VMEM((DATES * HALO, per_date * LANES), bf16),
            pltpu.VMEM((DATES // PACK, 2, ROWS, LANES), bf16),
            pltpu.VMEM((DATES, 2, ROWS, LANES), bf16),
            pltpu.VMEM(both.shape, bf16),
            pltpu.VMEM(pick.shape, bf16),
            pltpu.VMEM(order.shape, bf16),
            pltpu.VMEM(spread.shape, bf16),
            pltpu.VMEM(mask.shape, bf16),
            pltpu.VMEM((DATES, 2, ROWS, columns), f32),
            pltpu.VMEM((DATES, 2, ROWS, columns), bf16),
            pltpu.VMEM((2 * CHUNK * ROWS, columns), f32),
            pltpu.VMEM((GROUPS, SUB, columns), f32),
            pltpu.VMEM((GROUPS, DATES, DATES, 3, SUB, columns), f32),
            pltpu.VMEM((2, DATES, 3, SUB, columns), f32),
            pltpu.VMEM((TURNS, DATES, TURN * 2 * SUB, columns), bf16),
            pltpu.SemaphoreType.DMA((9,)),
        ] + [sems] * 6,
        compiler_params=pltpu.CompilerParams(
            collective_id=0, has_side_effects=True, vmem_limit_bytes=60 * 1024 * 1024
        ),
        name="link",
    )(ref_date, slcs, both, pick, order, spread, mask)

    if per_date > 1:
        table = lax.dynamic_index_in_dim(table, lax.rem(lax.axis_index("pix"), per_date), 0, False)
    else:
        table = table[0]
    parts = 4
    return pl.pallas_call(
        spectrum_kernel,
        out_shape=(
            jax.ShapeDtypeStruct((2, local_rows, strip_columns), f32),
            jax.ShapeDtypeStruct((2, ROWS, columns), f32),
        ),
        in_specs=[anywhere, vmem, vmem],
        out_specs=(anywhere, vmem),
        scratch_shapes=[
            pltpu.VMEM((devices, TURNS, TURN * 2 * SUB, columns), bf16),
            pltpu.VMEM((2, local_rows, strip_columns), f32),
            pltpu.SemaphoreType.DMA((parts,)),
            pltpu.SemaphoreType.DMA((parts,)),
        ],
        name="spectrum",
    )(phases, table, compressed)


def solution(mesh):
    return jax.shard_map(
        on_device,
        mesh=mesh,
        in_specs=(P(None, ("grp", "pix"), None), P("grp")),
        out_specs=(P(None, ("grp", "pix"), None), P(None, None, ("grp", "pix"))),
        check_vma=False,
    )
```

time: 57.8 us -> 48.4 us (0.84)
  Pallas kernels: 50.5 us -> 46.9 us
  local copies, waits for them, and re-layouts: 3.51 us -> 0 us
  other arithmetic: 2.25 us -> 0 us
    pallas_call x1, Pallas kernels: 50.5 us -> 42.9 us  [on_device(): pl.pallas_call(functools.partial(link_kernel, devices), out_shape=(jax.Sh...]
    pallas_call x0 -> x1, Pallas kernels: none -> 3.95 us  [on_device(): pl.pallas_call(spectrum_kernel, out_shape=(jax.ShapeDtypeStruct((2, local...]
    convert_element_type x1 -> x0, other arithmetic: 2.15 us -> none  [on_device(): return (spectrum.astype(jnp.float32), compressed)]
    unnamed x4 -> x0, local copies, waits for them, and re-layouts: 2.15 us -> none
    reshape x1 -> x0, local copies, waits for them, and re-layouts: 0.97 us -> none  [on_device(): halo = halo.reshape(devices, 2 * lines, LANES)]
where the time goes in v1:
time: 48.4 us; the launch traced here: 48.1 us
  Pallas kernels  46.9 us (97%)
  between operations  1.28 us (3%)
    pallas_call x1, Pallas kernels, on_device(): pl.pallas_call(functools.partial(link_kernel, devices), out_shape=(jax.Sh...  42.9 us
    pallas_call x1, Pallas kernels, on_device(): pl.pallas_call(spectrum_kernel, out_shape=(jax.ShapeDtypeStruct((2, local...  3.95 us

profile of v1, /device:TPU:0, one launch (start us, length us, event | category | flops | bytes accessed | tf_op | source)
XLA Modules:
  0.0 48.1 jit_solution(8503615394215370982)
XLA Ops:
  1.3 42.9 %link.1 = (bf16[16,4,32,128]{3,2,1,0:T(8,128)(2,1)}, f32[2,8,8,128]{3,2,1,0:T(8,128)}) custom-call(s32[1]{0:T(128)S(6)} %copy.10.ref_ref, bf16[2,64,2048]{2,1,0:T(8,128)(2,1)} %x_ref.1, bf16[256,128]{1,0:T(8,128)(2,1)} %constant.12.clone.both_ref, bf16[16,256]{1,0:T(8,128)(2,1)} %constant.13.clone.pick_ref, bf16[128,128]{1,0:T(8,128)(2,1)} %constant.14.clone.order_ref, ...), custom_call_target="tpu_custom_call" | custom-call | tf_op jit(solution)/shard_map/link/pallas_call | solution.py:442
  44.2 3.9 %spectrum.1 = (f32[2,64,2048]{2,1,0:T(8,128)}, f32[2,64,128]{2,1,0:T(8,128)}) custom-call(bf16[16,4,32,128]{3,2,1,0:T(8,128)(2,1)} %get-tuple-element.4.got_ref, bf16[128,256]{1,0:T(8,128)(2,1)} %constant.19.table_ref, f32[2,8,8,128]{3,2,1,0:T(8,128)} %get-tuple-element.5.comp_ref), custom_call_target="tpu_custom_call" | custom-call | tf_op jit(solution)/shard_map/spectrum/pallas_call | solution.py:483

commit v2 on v1

v2 whole, which is shorter than its diff:
```python
import functools
import math

import jax
import jax.numpy as jnp
import numpy as np
from jax import lax
from jax.experimental import pallas as pl
from jax.experimental.pallas import tpu as pltpu
from jax.sharding import PartitionSpec as P

DATES = 16
ROWS = 64
HALF_X = 5
HALF_Y = 2
POWER_ITERS = 6
LOADING = 0.25

LANES = 128
SUB = 8
GROUPS = ROWS // SUB
HALO = 16
PACK = LANES // HALO
CHUNK = 4
SPAN = 8
SCALE = 2.0 ** -6
MESH = pl.DeviceIdType.MESH


def window_weights(columns):
    target = np.arange(columns)[None, :]
    band = np.abs(np.arange(columns)[:, None] - target) <= HALF_X
    outside = np.concatenate([np.arange(-HALF_X, 0), columns + np.arange(HALF_X)])
    halo = np.zeros((HALO, columns), np.float32)
    halo[: 2 * HALF_X] = np.abs(outside[:, None] - target) <= HALF_X
    both = np.concatenate([band.astype(np.float32), np.tile(halo, (PACK, 1))], axis=0)
    return jnp.asarray(both * SCALE, jnp.bfloat16)


def pick_weights(columns):
    pick = np.zeros((HALO, 2 * columns), np.float32)
    for h in range(HALF_X):
        pick[h, columns - HALF_X + h] = 1.0
        pick[HALF_X + h, columns + h] = 1.0
    return jnp.asarray(pick, jnp.bfloat16)


def order_weights(local_rows):
    per_date = ROWS // local_rows
    order = np.zeros((2, GROUPS, SUB, per_date, LANES), np.float32)
    for c in range(2):
        for line in range(ROWS):
            q, r = divmod(line, local_rows)
            order[c, line % GROUPS, line // GROUPS, q, c * local_rows + r] = 1.0
    return jnp.asarray(order.reshape(2 * ROWS, per_date * LANES), jnp.bfloat16)


def block_masks():
    block = np.arange(PACK)[:, None, None] == (np.arange(LANES) // HALO)[None, None, :]
    return jnp.asarray(np.broadcast_to(block, (PACK, 2 * SUB, LANES)), jnp.float32)


def dct_weights(local_rows):
    frequency = np.arange(ROWS, dtype=np.float64)[:, None]
    position = np.arange(ROWS, dtype=np.float64)[None, :]
    weight = np.where(frequency == 0, math.sqrt(1.0 / ROWS), math.sqrt(2.0 / ROWS))
    table = weight * np.cos(np.pi * (2.0 * position + 1.0) * frequency / (2.0 * ROWS))
    table = table.reshape(ROWS // local_rows, local_rows, SUB, GROUPS).transpose(0, 1, 3, 2)
    big = np.zeros((ROWS // local_rows, 2, local_rows, GROUPS, 2, SUB), np.float32)
    for c in range(2):
        big[:, c, :, :, c] = table
    big = big.reshape(ROWS // local_rows, 2 * local_rows, 2 * ROWS)
    high = big.astype(jnp.bfloat16)
    low = (big - high.astype(np.float32)).astype(jnp.bfloat16)
    return jnp.asarray(np.concatenate([high, low], axis=2))


def pair_products(one, two):
    real = one[0] * two[0] + one[1] * two[1]
    imag = one[1] * two[0] - one[0] * two[1]
    return real, imag


def tall_of(value, rows):
    return jnp.concatenate([value] * (rows // value.shape[0]), axis=0)


def flips(a, size):
    out, bit = [], 1
    while bit < size:
        out.append(bit - 2 * bit * ((a // bit) % 2))
        bit *= 2
    return out


def flipped(a, deltas, b):
    for n, delta in enumerate(deltas):
        if isinstance(b, int):
            a = a + delta if (b >> n) & 1 else a
        else:
            a = a + delta * ((b // (1 << n)) % 2)
    return a


def link_kernel(devices, ref_ref, x_ref, both_ref, pick_ref, order_ref, mask_ref,
                o_ref, comp_ref,
                xs, win, hsend, hwin, edge, wide, both, pick, order, mask,
                stage, zb, summed, load, cov, vec, tile, comp,
                local, ssem, rsem, hs, hr, ts, tr):
    columns = win.shape[3]
    local_rows = win.shape[2]
    strip_columns = x_ref.shape[2]
    per_date = ROWS // local_rows
    me = lax.axis_index("pix")
    my_date = me // per_date
    turns = flips(me, devices)
    date_turns = turns[(per_date - 1).bit_length():]
    peers = [flipped(me, turns, off) for off in range(devices)]
    bf16, f32 = jnp.bfloat16, jnp.float32

    barrier = pltpu.get_barrier_semaphore()
    for peer in peers[1:]:
        pl.semaphore_signal(barrier, inc=1, device_id={"pix": peer}, device_id_type=MESH)

    def block(n):
        return x_ref.at[:, :, pl.ds(pl.multiple_of(n * columns, columns), columns)]

    loads = [
        pltpu.make_async_copy(src, dst, local.at[n])
        for n, (src, dst) in enumerate((
            (x_ref, xs.at[:, :, columns:columns + strip_columns]),
            (pick_ref, pick), (block(me), win.at[me]), (both_ref, both), (order_ref, order),
            (mask_ref, mask),
        ))
    ]
    for copy in loads:
        copy.start()

    def main_copy(off, peer):
        return pltpu.make_async_remote_copy(
            src_ref=block(peer), dst_ref=win.at[me], send_sem=ssem.at[off], recv_sem=rsem.at[off],
            device_id={"pix": peer}, device_id_type=MESH,
        )

    def halo_copy(off, peer):
        return pltpu.make_async_remote_copy(
            src_ref=hsend.at[peer], dst_ref=hwin.at[me], send_sem=hs.at[off],
            recv_sem=hr.at[off], device_id={"pix": peer}, device_id_type=MESH,
        )

    first = sorted({1, 2, 3, devices // 4, 3 * devices // 4, 3 * devices // 4 + 1})
    later = [off for off in range(1, devices) if off not in first]
    halos = [halo_copy(off, peers[off]) for off in range(1, devices)]
    mains = {off: main_copy(off, peers[off]) for off in range(1, devices)}

    pl.semaphore_wait(barrier, devices - 1)
    for off in first:
        mains[off].start()

    margin = jnp.zeros((2, local_rows, columns), bf16)
    xs[:, :, 0:columns] = margin
    xs[:, :, columns + strip_columns:2 * columns + strip_columns] = margin
    loads[0].wait()
    loads[1].wait()

    blocks = min(devices, 16)

    def cut_halos(n, carry):
        for q in range(blocks):
            at = (n * blocks + q) * columns
            left = xs[:, :, pl.ds(pl.multiple_of(at, columns), columns)]
            right = xs[:, :, pl.ds(pl.multiple_of(at + 2 * columns, columns), columns)]
            near = jnp.concatenate(
                [left.reshape(2 * local_rows, columns), right.reshape(2 * local_rows, columns)], axis=1
            )
            if 2 * local_rows < LANES:
                fill = jnp.zeros((LANES - 2 * local_rows, 2 * columns), bf16)
                near = jnp.concatenate([near, fill], axis=0)
            got = lax.dot_general(
                pick[...], near, (((1,), (1,)), ((), ())), preferred_element_type=f32
            )
            hsend[n * blocks + q] = got.astype(bf16)
        return carry

    lax.fori_loop(0, devices // blocks, cut_halos, 0)
    hwin[me] = hsend[me]
    for c in halos:
        c.start()
    for off in later:
        mains[off].start()

    first_column = me * columns
    sub = lax.broadcasted_iota(jnp.int32, (SUB, columns), 0)
    lane = lax.broadcasted_iota(jnp.int32, (SUB, columns), 1) + first_column
    across = jnp.minimum(lane + HALF_X, strip_columns - 1) - jnp.maximum(lane - HALF_X, 0) + 1
    for g in range(GROUPS):
        line = sub * GROUPS + g
        along = jnp.minimum(line + HALF_Y, ROWS - 1) - jnp.maximum(line - HALF_Y, 0) + 1
        load[g] = (along * across).astype(f32) * (LOADING * SCALE)
    edge[...] = jnp.zeros_like(edge)
    for copy in loads[2:]:
        copy.wait()

    def date_at(p):
        return flipped(my_date, date_turns, p)

    def tall(value):
        return tall_of(value, ROWS)

    def window_sums(plane):
        rows = [plane[g * SUB:(g + 1) * SUB] for g in range(GROUPS)]
        before = [jnp.where(sub == 0, 0.0, pltpu.roll(x, 1, 0)) for x in rows[-HALF_Y:]]
        after = [jnp.where(sub == SUB - 1, 0.0, pltpu.roll(x, SUB - 1, 0)) for x in rows[:HALF_Y]]
        ext = before + rows + after
        two = [ext[2 * k] + ext[2 * k + 1] for k in range(GROUPS // 2 + 2)]
        four = [two[k] + two[k + 1] for k in range(GROUPS // 2 + 1)]
        out = []
        for k in range(GROUPS // 2):
            out.append(four[k] + ext[2 * k + 4])
            out.append(ext[2 * k + 1] + four[k + 1])
        return out

    def finish(p, n):
        for q in range(CHUNK):
            sums = [
                window_sums(summed[(2 * q + part) * ROWS:(2 * q + part + 1) * ROWS])
                for part in range(2)
            ]
            for g in range(GROUPS):
                real, imag = sums[0][g], sums[1][g]
                cov[g, p, n * CHUNK + q, 0] = real
                cov[g, p, n * CHUNK + q, 1] = real + imag
                cov[g, p, n * CHUNK + q, 2] = imag - real

    def begin(p, n):
        one = zb[p, 0].astype(bf16), zb[p, 1].astype(bf16)
        half = (n * CHUNK) // PACK
        margins = pair_products(
            (wide[0].astype(bf16), wide[1].astype(bf16)),
            (edge[half, 0].astype(bf16), edge[half, 1].astype(bf16)),
        )
        planes = []
        for q in range(CHUNK):
            k = n * CHUNK + q
            two = zb[k, 0].astype(bf16), zb[k, 1].astype(bf16)
            keep = tall(mask[k - half * PACK].astype(bf16))
            for value, margin in zip(pair_products(one, two), margins):
                planes.append(jnp.concatenate([value, margin * keep], axis=1))
        summed[...] = jnp.dot(
            jnp.concatenate(planes, axis=0), both[...], preferred_element_type=f32
        )

    def covariances(p, prev):
        sources = []
        for q in range(per_date):
            off = p * per_date + q
            source = flipped(me, turns, off)
            sources.append(source)

            @pl.when(off != 0)
            def _():
                pltpu.make_async_remote_copy(
                    src_ref=hsend.at[source], dst_ref=hwin.at[source], send_sem=hs.at[off],
                    recv_sem=hr.at[off], device_id={"pix": source}, device_id_type=MESH,
                ).wait_recv()
                pltpu.make_async_remote_copy(
                    src_ref=block(source), dst_ref=win.at[source], send_sem=ssem.at[off],
                    recv_sem=rsem.at[off], device_id={"pix": source}, device_id_type=MESH,
                ).wait_recv()

        sources = [date_at(p) * per_date + q for q in range(per_date)]
        margin = jnp.concatenate([tall_of(hwin[source], LANES) for source in sources], axis=1)
        got = lax.dot_general(
            order[...], margin, (((1,), (1,)), ((), ())), preferred_element_type=f32
        )
        keep = tall(mask[lax.rem(p, PACK)])
        half = p // PACK
        for c in range(2):
            part = got[c * ROWS:(c + 1) * ROWS]
            wide[c] = part
            edge[half, c] = edge[half, c] + part * keep
        for q, source in enumerate(sources):
            for c in range(2):
                stage[c, q * local_rows:(q + 1) * local_rows] = win[source, c].astype(f32)
        for c in range(2):
            for g in range(GROUPS):
                zb[p, c, g * SUB:(g + 1) * SUB] = stage[c, pl.ds(g, SUB, stride=GROUPS), :]

        def chunk(n, prev):
            finish(*prev)
            begin(p, n)
            return p, n

        return lax.fori_loop(0, p // CHUNK + 1, chunk, prev)

    finish(*lax.fori_loop(0, DATES, covariances, (jnp.int32(0), jnp.int32(0))))

    ref = flipped(my_date, date_turns, ref_ref[0])

    def send(g):
        for off in range(1, devices):
            pltpu.make_async_remote_copy(
                src_ref=tile.at[g, off // per_date], dst_ref=o_ref.at[me, g],
                send_sem=ts.at[off], recv_sem=tr.at[off],
                device_id={"pix": peers[off]}, device_id_type=MESH,
            ).start()
        pltpu.make_async_copy(tile.at[g, 0], o_ref.at[me, g], local.at[6]).start()

    def solve(g, carry):
        for i in range(DATES):
            cov[g, i, i, 0] = cov[g, i, i, 0] + load[g]
        for i in range(DATES):
            one, two = jnp.maximum(ref, i), jnp.minimum(ref, i)
            real = cov[g, one, two, 0]
            imag = 0.5 * (cov[g, one, two, 1] + cov[g, one, two, 2])
            sign = jnp.where(ref == i, 0.0, jnp.where(ref < i, 1.0, -1.0))
            imag = imag * sign
            vec[0, i, 0] = real
            vec[0, i, 1] = imag
            vec[0, i, 2] = real + imag

        @pl.when(g > 0)
        def _():
            send(g - 1)

        def step(t, carry):
            src = lax.rem(t, 2)
            for base in range(0, DATES, SPAN):
                acc = [[None] * 3 for _ in range(SPAN)]
                for j in range(DATES):
                    vr, vi, vs = vec[src, j, 0], vec[src, j, 1], vec[src, j, 2]
                    for q in range(SPAN):
                        i = base + q
                        one, two = max(i, j), min(i, j)
                        cr = cov[g, one, two, 0]
                        if i == j:
                            terms, minus = (None, cr * vr, cr * vi), (False, True, False)
                        elif i > j:
                            terms = (cr * vs, cov[g, i, j, 1] * vi, cov[g, i, j, 2] * vr)
                            minus = (False, False, False)
                        else:
                            terms = (cr * vs, cov[g, j, i, 2] * vi, cov[g, j, i, 1] * vr)
                            minus = (False, True, True)
                        for n in range(3):
                            if terms[n] is None:
                                continue
                            if acc[q][n] is None:
                                acc[q][n] = -terms[n] if minus[n] else terms[n]
                            elif minus[n]:
                                acc[q][n] = acc[q][n] - terms[n]
                            else:
                                acc[q][n] = acc[q][n] + terms[n]
                for q in range(SPAN):
                    real, imag = acc[q][0] - acc[q][1], acc[q][0] + acc[q][2]
                    vec[1 - src, base + q, 0] = real
                    vec[1 - src, base + q, 1] = imag
                    vec[1 - src, base + q, 2] = real + imag
            return carry

        lax.fori_loop(0, POWER_ITERS - 1, step, 0)
        last = (POWER_ITERS - 1) % 2
        total = jnp.zeros((SUB, columns), f32)
        for k in range(DATES):
            vr, vi = vec[last, k, 0], vec[last, k, 1]
            total = total + (vr * vr + vi * vi)
        scale = DATES / total
        rr, ri = vec[last, ref, 0] * scale, vec[last, ref, 1] * scale
        comp_r = jnp.zeros_like(total)
        comp_i = jnp.zeros_like(total)
        at = pl.ds(pl.multiple_of(g * SUB, SUB), SUB)
        for k in range(DATES):
            vr, vi = vec[last, k, 0], vec[last, k, 1]
            lr = vr * rr + vi * ri
            li = vi * rr - vr * ri
            zr, zi = zb[k, 0, at], zb[k, 1, at]
            comp_r = comp_r + (lr * zr + li * zi)
            comp_i = comp_i + (lr * zi - li * zr)
            tile[g, k] = jnp.concatenate([lr, li], axis=0).astype(bf16)
        comp[0, g] = comp_r * (1.0 / math.sqrt(DATES))
        comp[1, g] = comp_i * (1.0 / math.sqrt(DATES))
        return carry

    lax.fori_loop(0, GROUPS, solve, 0)
    for c in halos:
        c.wait_send()
    send(GROUPS - 1)
    out = pltpu.make_async_copy(comp, comp_ref, local.at[7])
    out.start()
    for off in range(1, devices):
        mains[off].wait_send()

    whole = tile.at[:, 0]
    for off in range(1, devices):
        pltpu.make_async_remote_copy(
            src_ref=whole, dst_ref=o_ref.at[me], send_sem=ts.at[off], recv_sem=tr.at[off],
            device_id={"pix": peers[off]}, device_id_type=MESH,
        ).wait()
    pltpu.make_async_copy(whole, o_ref.at[me], local.at[6]).wait()
    out.wait()


def spectrum_kernel(got_ref, table_ref, comp_ref, o_ref, out_ref, got, table, comp, order, out, ins, outs):
    devices, columns = got.shape[0], got.shape[3]
    local_rows = out.shape[1]
    parts = outs.shape[0] - 1
    size = devices // parts

    def copy_in(n):
        at = pl.ds(n * size, size)
        return pltpu.make_async_copy(got_ref.at[at], got.at[at], ins.at[n])

    def copy_out(n):
        at = pl.ds(n * size * columns, size * columns)
        return pltpu.make_async_copy(out.at[:, :, at], o_ref.at[:, :, at], outs.at[n])

    tables = pltpu.make_async_copy(table_ref, table, ins.at[parts])
    comps = pltpu.make_async_copy(comp_ref, comp, ins.at[parts + 1])
    tables.start()
    for n in range(parts):
        copy_in(n).start()
    comps.start()
    tables.wait()
    for n in range(parts):
        copy_in(n).wait()
        for m in range(0, size, 2):
            at = n * size + m
            both = jnp.concatenate(
                [got[at].reshape(2 * ROWS, columns), got[at + 1].reshape(2 * ROWS, columns)], axis=1
            )
            value = jnp.dot(
                table[...], jnp.concatenate([both, both], axis=0), preferred_element_type=jnp.float32
            )
            for c in range(2):
                out[c, :, at * columns:(at + 2) * columns] = value[c * local_rows:(c + 1) * local_rows]
        copy_out(n).start()
    comps.wait()
    for c in range(2):
        for g in range(GROUPS):
            order[c, pl.ds(g, SUB, stride=GROUPS), :] = comp[c, g]
    last = pltpu.make_async_copy(order, out_ref, outs.at[parts])
    last.start()
    for n in range(parts):
        copy_out(n).wait()
    last.wait()


def on_device(slcs, ref_date):
    devices = lax.axis_size("pix")
    local_rows, strip_columns = slcs.shape[1], slcs.shape[2]
    columns = strip_columns // devices
    per_date = ROWS // local_rows

    anywhere = pl.BlockSpec(memory_space=pl.ANY)
    both, pick, order = window_weights(columns), pick_weights(columns), order_weights(local_rows)
    mask = block_masks()
    table = dct_weights(local_rows)
    f32, bf16 = jnp.float32, jnp.bfloat16
    sems = pltpu.SemaphoreType.DMA((devices,))
    phases, compressed = pl.pallas_call(
        functools.partial(link_kernel, devices),
        out_shape=(
            jax.ShapeDtypeStruct((devices, GROUPS, 2 * SUB, columns), bf16),
            jax.ShapeDtypeStruct((2, GROUPS, SUB, columns), f32),
        ),
        in_specs=[pl.BlockSpec(memory_space=pltpu.SMEM)] + [anywhere] * 5,
        out_specs=(anywhere, anywhere),
        scratch_shapes=[
            pltpu.VMEM((2, local_rows, strip_columns + 2 * columns), bf16),
            pltpu.VMEM((devices, 2, local_rows, columns), bf16),
            pltpu.VMEM((devices, HALO, LANES), bf16),
            pltpu.VMEM((devices, HALO, LANES), bf16),
            pltpu.VMEM((DATES // PACK, 2, ROWS, LANES), f32),
            pltpu.VMEM((2, ROWS, LANES), f32),
            pltpu.VMEM(both.shape, bf16),
            pltpu.VMEM(pick.shape, bf16),
            pltpu.VMEM(order.shape, bf16),
            pltpu.VMEM(mask.shape, f32),
            pltpu.VMEM((2, ROWS, columns), f32),
            pltpu.VMEM((DATES, 2, ROWS, columns), f32),
            pltpu.VMEM((2 * CHUNK * ROWS, columns), f32),
            pltpu.VMEM((GROUPS, SUB, columns), f32),
            pltpu.VMEM((GROUPS, DATES, DATES, 3, SUB, columns), f32),
            pltpu.VMEM((2, DATES, 3, SUB, columns), f32),
            pltpu.VMEM((GROUPS, DATES, 2 * SUB, columns), bf16),
            pltpu.VMEM((2, GROUPS, SUB, columns), f32),
            pltpu.SemaphoreType.DMA((8,)),
        ] + [sems] * 6,
        compiler_params=pltpu.CompilerParams(
            collective_id=0, has_side_effects=True, vmem_limit_bytes=60 * 1024 * 1024
        ),
        name="link",
    )(ref_date, slcs, both, pick, order, mask)

    if per_date > 1:
        table = lax.dynamic_index_in_dim(table, lax.rem(lax.axis_index("pix"), per_date), 0, False)
    else:
        table = table[0]
    parts = 4
    return pl.pallas_call(
        spectrum_kernel,
        out_shape=(
            jax.ShapeDtypeStruct((2, local_rows, strip_columns), f32),
            jax.ShapeDtypeStruct((2, ROWS, columns), f32),
        ),
        in_specs=[anywhere] * 3,
        out_specs=(anywhere, anywhere),
        scratch_shapes=[
            pltpu.VMEM((devices, GROUPS, 2 * SUB, columns), bf16),
            pltpu.VMEM(table.shape, bf16),
            pltpu.VMEM((2, GROUPS, SUB, columns), f32),
            pltpu.VMEM((2, ROWS, columns), f32),
            pltpu.VMEM((2, local_rows, strip_columns), f32),
            pltpu.SemaphoreType.DMA((parts + 2,)),
            pltpu.SemaphoreType.DMA((parts + 1,)),
        ],
        name="spectrum",
    )(phases, table, compressed)


def solution(mesh):
    return jax.shard_map(
        on_device,
        mesh=mesh,
        in_specs=(P(None, ("grp", "pix"), None), P("grp")),
        out_specs=(P(None, ("grp", "pix"), None), P(None, None, ("grp", "pix"))),
        check_vma=False,
    )
```

time: 48.4 us -> 46.9 us (0.969)
  Pallas kernels: 46.9 us -> 45.4 us
    pallas_call x1, Pallas kernels: 3.95 us -> 2.53 us  [on_device(): pl.pallas_call(spectrum_kernel, out_shape=(jax.ShapeDtypeStruct((2, local...]
where the time goes in v2:
time: 46.9 us; the launch traced here: 46.7 us
  Pallas kernels  45.4 us (97%)
  between operations  1.28 us (3%)
    pallas_call x1, Pallas kernels, on_device(): pl.pallas_call(functools.partial(link_kernel, devices), out_shape=(jax.Sh...  42.9 us
    pallas_call x1, Pallas kernels, on_device(): pl.pallas_call(spectrum_kernel, out_shape=(jax.ShapeDtypeStruct((2, local...  2.53 us

profile of v2, /device:TPU:0, one launch (start us, length us, event | category | flops | bytes accessed | tf_op | source)
XLA Modules:
  0.0 46.7 jit_solution(6724159935689389318)
XLA Ops:
  1.3 42.9 %link.1 = (bf16[16,8,16,128]{3,2,1,0:T(8,128)(2,1)}, f32[2,8,8,128]{3,2,1,0:T(8,128)}) custom-call(s32[1]{0:T(128)S(6)} %copy.9.ref_ref, bf16[2,64,2048]{2,1,0:T(8,128)(2,1)} %x_ref.1, bf16[256,128]{1,0:T(8,128)(2,1)} %constant.10.clone.both_ref, bf16[16,256]{1,0:T(8,128)(2,1)} %constant.11.clone.pick_ref, bf16[128,128]{1,0:T(8,128)(2,1)} %constant.12.clone.order_ref, ...), custom_call_target="tpu_custom_call" | custom-call | tf_op jit(solution)/shard_map/link/pallas_call | solution.py:459
  44.2 2.5 %spectrum.1 = (f32[2,64,2048]{2,1,0:T(8,128)}, f32[2,64,128]{2,1,0:T(8,128)}) custom-call(bf16[16,8,16,128]{3,2,1,0:T(8,128)(2,1)} %get-tuple-element.4.got_ref, bf16[128,256]{1,0:T(8,128)(2,1)} %constant.16.table_ref, f32[2,8,8,128]{3,2,1,0:T(8,128)} %get-tuple-element.5.comp_ref), custom_call_target="tpu_custom_call" | custom-call | tf_op jit(solution)/shard_map/spectrum/pallas_call | solution.py:499

commit v3 on v2

--- a/solution.py
+++ b/solution.py
@@ -21,7 +21,7 @@
 GROUPS = ROWS // SUB
 HALO = 16
 PACK = LANES // HALO
-CHUNK = 4
+CHUNK = 8
 SPAN = 8
 SCALE = 2.0 ** -6
 MESH = pl.DeviceIdType.MESH
@@ -104,12 +104,13 @@
 
 def link_kernel(devices, ref_ref, x_ref, both_ref, pick_ref, order_ref, mask_ref,
                 o_ref, comp_ref,
-                xs, win, hsend, hwin, edge, wide, both, pick, order, mask,
+                xs, win, hsend, edge, wide, both, pick, order, mask,
                 stage, zb, summed, load, cov, vec, tile, comp,
-                local, ssem, rsem, hs, hr, ts, tr):
-    columns = win.shape[3]
-    local_rows = win.shape[2]
-    strip_columns = x_ref.shape[2]
+                local, sent, rsem, got_sem):
+    columns = win.shape[2]
+    height = x_ref.shape[0]
+    local_rows = height // 2
+    strip_columns = x_ref.shape[1]
     per_date = ROWS // local_rows
     me = lax.axis_index("pix")
     my_date = me // per_date
@@ -123,13 +124,13 @@
         pl.semaphore_signal(barrier, inc=1, device_id={"pix": peer}, device_id_type=MESH)
 
     def block(n):
-        return x_ref.at[:, :, pl.ds(pl.multiple_of(n * columns, columns), columns)]
+        return x_ref.at[:, pl.ds(pl.multiple_of(n * columns, columns), columns)]
 
     loads = [
         pltpu.make_async_copy(src, dst, local.at[n])
         for n, (src, dst) in enumerate((
-            (x_ref, xs.at[:, :, columns:columns + strip_columns]),
-            (pick_ref, pick), (block(me), win.at[me]), (both_ref, both), (order_ref, order),
+            (x_ref, xs.at[:, columns:columns + strip_columns]),
+            (pick_ref, pick), (block(me), win.at[me, 0:height]), (both_ref, both), (order_ref, order),
             (mask_ref, mask),
         ))
     ]
@@ -138,14 +139,14 @@
 
     def main_copy(off, peer):
         return pltpu.make_async_remote_copy(
-            src_ref=block(peer), dst_ref=win.at[me], send_sem=ssem.at[off], recv_sem=rsem.at[off],
-            device_id={"pix": peer}, device_id_type=MESH,
+            src_ref=block(peer), dst_ref=win.at[me, 0:height], send_sem=sent.at[0],
+            recv_sem=rsem.at[off], device_id={"pix": peer}, device_id_type=MESH,
         )
 
     def halo_copy(off, peer):
         return pltpu.make_async_remote_copy(
-            src_ref=hsend.at[peer], dst_ref=hwin.at[me], send_sem=hs.at[off],
-            recv_sem=hr.at[off], device_id={"pix": peer}, device_id_type=MESH,
+            src_ref=hsend.at[peer], dst_ref=win.at[me, height:height + HALO], send_sem=sent.at[0],
+            recv_sem=rsem.at[off], device_id={"pix": peer}, device_id_type=MESH,
         )
 
     first = sorted({1, 2, 3, devices // 4, 3 * devices // 4, 3 * devices // 4 + 1})
@@ -157,9 +158,9 @@
     for off in first:
         mains[off].start()
 
-    margin = jnp.zeros((2, local_rows, columns), bf16)
-    xs[:, :, 0:columns] = margin
-    xs[:, :, columns + strip_columns:2 * columns + strip_columns] = margin
+    margin = jnp.zeros((height, columns), bf16)
+    xs[:, 0:columns] = margin
+    xs[:, columns + strip_columns:2 * columns + strip_columns] = margin
     loads[0].wait()
     loads[1].wait()
 
@@ -168,13 +169,11 @@
     def cut_halos(n, carry):
         for q in range(blocks):
             at = (n * blocks + q) * columns
-            left = xs[:, :, pl.ds(pl.multiple_of(at, columns), columns)]
-            right = xs[:, :, pl.ds(pl.multiple_of(at + 2 * columns, columns), columns)]
-            near = jnp.concatenate(
-                [left.reshape(2 * local_rows, columns), right.reshape(2 * local_rows, columns)], axis=1
-            )
-            if 2 * local_rows < LANES:
-                fill = jnp.zeros((LANES - 2 * local_rows, 2 * columns), bf16)
+            left = xs[:, pl.ds(pl.multiple_of(at, columns), columns)]
+            right = xs[:, pl.ds(pl.multiple_of(at + 2 * columns, columns), columns)]
+            near = jnp.concatenate([left, right], axis=1)
+            if height < LANES:
+                fill = jnp.zeros((LANES - height, 2 * columns), bf16)
                 near = jnp.concatenate([near, fill], axis=0)
             got = lax.dot_general(
                 pick[...], near, (((1,), (1,)), ((), ())), preferred_element_type=f32
@@ -183,7 +182,7 @@
         return carry
 
     lax.fori_loop(0, devices // blocks, cut_halos, 0)
-    hwin[me] = hsend[me]
+    win[me, height:height + HALO] = hsend[me]
     for c in halos:
         c.start()
     for off in later:
@@ -251,25 +250,19 @@
         )
 
     def covariances(p, prev):
-        sources = []
         for q in range(per_date):
             off = p * per_date + q
             source = flipped(me, turns, off)
-            sources.append(source)
 
             @pl.when(off != 0)
             def _():
                 pltpu.make_async_remote_copy(
-                    src_ref=hsend.at[source], dst_ref=hwin.at[source], send_sem=hs.at[off],
-                    recv_sem=hr.at[off], device_id={"pix": source}, device_id_type=MESH,
-                ).wait_recv()
-                pltpu.make_async_remote_copy(
-                    src_ref=block(source), dst_ref=win.at[source], send_sem=ssem.at[off],
+                    src_ref=win.at[source], dst_ref=win.at[source], send_sem=sent.at[0],
                     recv_sem=rsem.at[off], device_id={"pix": source}, device_id_type=MESH,
                 ).wait_recv()
 
         sources = [date_at(p) * per_date + q for q in range(per_date)]
-        margin = jnp.concatenate([tall_of(hwin[source], LANES) for source in sources], axis=1)
+        margin = jnp.concatenate([tall_of(win[source, height:height + HALO], LANES) for source in sources], axis=1)
         got = lax.dot_general(
             order[...], margin, (((1,), (1,)), ((), ())), preferred_element_type=f32
         )
@@ -281,7 +274,9 @@
             edge[half, c] = edge[half, c] + part * keep
         for q, source in enumerate(sources):
             for c in range(2):
-                stage[c, q * local_rows:(q + 1) * local_rows] = win[source, c].astype(f32)
+                stage[c, q * local_rows:(q + 1) * local_rows] = win[
+                    source, c * local_rows:(c + 1) * local_rows
+                ].astype(f32)
         for c in range(2):
             for g in range(GROUPS):
                 zb[p, c, g * SUB:(g + 1) * SUB] = stage[c, pl.ds(g, SUB, stride=GROUPS), :]
@@ -301,7 +296,7 @@
         for off in range(1, devices):
             pltpu.make_async_remote_copy(
                 src_ref=tile.at[g, off // per_date], dst_ref=o_ref.at[me, g],
-                send_sem=ts.at[off], recv_sem=tr.at[off],
+                send_sem=sent.at[1], recv_sem=got_sem.at[0],
                 device_id={"pix": peers[off]}, device_id_type=MESH,
             ).start()
         pltpu.make_async_copy(tile.at[g, 0], o_ref.at[me, g], local.at[6]).start()
@@ -381,22 +376,20 @@
         return carry
 
     lax.fori_loop(0, GROUPS, solve, 0)
-    for c in halos:
-        c.wait_send()
+    pltpu.make_async_remote_copy(
+        src_ref=win.at[0:devices - 1], dst_ref=win.at[0:devices - 1], send_sem=sent.at[0],
+        recv_sem=rsem.at[0], device_id={"pix": peers[1]}, device_id_type=MESH,
+    ).wait_send()
     send(GROUPS - 1)
     out = pltpu.make_async_copy(comp, comp_ref, local.at[7])
     out.start()
-    for off in range(1, devices):
-        mains[off].wait_send()
-
-    whole = tile.at[:, 0]
-    for off in range(1, devices):
-        pltpu.make_async_remote_copy(
-            src_ref=whole, dst_ref=o_ref.at[me], send_sem=ts.at[off], recv_sem=tr.at[off],
-            device_id={"pix": peers[off]}, device_id_type=MESH,
-        ).wait()
-    pltpu.make_async_copy(whole, o_ref.at[me], local.at[6]).wait()
+    pltpu.make_async_copy(tile.at[:, 0], o_ref.at[me], local.at[6]).wait()
     out.wait()
+    others = o_ref.at[0:devices - 1]
+    pltpu.make_async_remote_copy(
+        src_ref=others, dst_ref=others, send_sem=sent.at[1], recv_sem=got_sem.at[0],
+        device_id={"pix": peers[1]}, device_id_type=MESH,
+    ).wait()
 
 
 def spectrum_kernel(got_ref, table_ref, comp_ref, o_ref, out_ref, got, table, comp, order, out, ins, outs):
@@ -455,7 +448,6 @@
     mask = block_masks()
     table = dct_weights(local_rows)
     f32, bf16 = jnp.float32, jnp.bfloat16
-    sems = pltpu.SemaphoreType.DMA((devices,))
     phases, compressed = pl.pallas_call(
         functools.partial(link_kernel, devices),
         out_shape=(
@@ -465,9 +457,8 @@
         in_specs=[pl.BlockSpec(memory_space=pltpu.SMEM)] + [anywhere] * 5,
         out_specs=(anywhere, anywhere),
         scratch_shapes=[
-            pltpu.VMEM((2, local_rows, strip_columns + 2 * columns), bf16),
-            pltpu.VMEM((devices, 2, local_rows, columns), bf16),
-            pltpu.VMEM((devices, HALO, LANES), bf16),
+            pltpu.VMEM((2 * local_rows, strip_columns + 2 * columns), bf16),
+            pltpu.VMEM((devices, 2 * local_rows + HALO, columns), bf16),
             pltpu.VMEM((devices, HALO, LANES), bf16),
             pltpu.VMEM((DATES // PACK, 2, ROWS, LANES), f32),
             pltpu.VMEM((2, ROWS, LANES), f32),
@@ -484,18 +475,21 @@
             pltpu.VMEM((GROUPS, DATES, 2 * SUB, columns), bf16),
             pltpu.VMEM((2, GROUPS, SUB, columns), f32),
             pltpu.SemaphoreType.DMA((8,)),
-        ] + [sems] * 6,
+            pltpu.SemaphoreType.DMA((2,)),
+            pltpu.SemaphoreType.DMA((devices,)),
+            pltpu.SemaphoreType.DMA((1,)),
+        ],
         compiler_params=pltpu.CompilerParams(
             collective_id=0, has_side_effects=True, vmem_limit_bytes=60 * 1024 * 1024
         ),
         name="link",
-    )(ref_date, slcs, both, pick, order, mask)
+    )(ref_date, slcs.reshape(2 * local_rows, strip_columns), both, pick, order, mask)
 
     if per_date > 1:
         table = lax.dynamic_index_in_dim(table, lax.rem(lax.axis_index("pix"), per_date), 0, False)
     else:
         table = table[0]
-    parts = 4
+    parts = 2
     return pl.pallas_call(
         spectrum_kernel,
         out_shape=(

time: 46.9 us -> 44.7 us (0.953)
  Pallas kernels: 45.4 us -> 43.2 us
    pallas_call x1, Pallas kernels: 42.9 us -> 40.9 us  [on_device(): pl.pallas_call(functools.partial(link_kernel, devices), out_shape=(jax.Sh...]
where the time goes in v3:
time: 44.7 us; the launch traced here: 44.5 us
  Pallas kernels  43.2 us (97%)
  between operations  1.28 us (3%)
    pallas_call x1, Pallas kernels, on_device(): pl.pallas_call(functools.partial(link_kernel, devices), out_shape=(jax.Sh...  40.9 us
    pallas_call x1, Pallas kernels, on_device(): pl.pallas_call(spectrum_kernel, out_shape=(jax.ShapeDtypeStruct((2, local...  2.33 us

profile of v3, /device:TPU:0, one launch (start us, length us, event | category | flops | bytes accessed | tf_op | source)
XLA Modules:
  0.0 44.5 jit_solution(17654012998234792304)
XLA Ops:
  1.3 40.9 %link.1 = (bf16[16,8,16,128]{3,2,1,0:T(8,128)(2,1)}, f32[2,8,8,128]{3,2,1,0:T(8,128)}) custom-call(s32[1]{0:T(128)S(6)} %copy.9.ref_ref, bf16[128,2048]{1,0:T(8,128)(2,1)} %bitcast.1, bf16[256,128]{1,0:T(8,128)(2,1)} %constant.10.clone.both_ref, bf16[16,256]{1,0:T(8,128)(2,1)} %constant.11.clone.pick_ref, bf16[128,128]{1,0:T(8,128)(2,1)} %constant.12.clone.order_ref, ...), custom_call_target="tpu_custom_call" | custom-call | tf_op jit(solution)/shard_map/link/pallas_call | solution.py:451
  42.2 2.3 %spectrum.1 = (f32[2,64,2048]{2,1,0:T(8,128)}, f32[2,64,128]{2,1,0:T(8,128)}) custom-call(bf16[16,8,16,128]{3,2,1,0:T(8,128)(2,1)} %get-tuple-element.4.got_ref, bf16[128,256]{1,0:T(8,128)(2,1)} %constant.16.table_ref, f32[2,8,8,128]{3,2,1,0:T(8,128)} %get-tuple-element.5.comp_ref), custom_call_target="tpu_custom_call" | custom-call | tf_op jit(solution)/shard_map/spectrum/pallas_call | solution.py:493

commit v4 on v3

--- a/solution.py
+++ b/solution.py
@@ -22,8 +22,11 @@
 HALO = 16
 PACK = LANES // HALO
 CHUNK = 8
+BATCH = 2
 SPAN = 8
 SCALE = 2.0 ** -6
+LINK_VMEM = 40 * 1024 * 1024
+SPECTRUM_VMEM = 12 * 1024 * 1024
 MESH = pl.DeviceIdType.MESH
 
 
@@ -149,7 +152,8 @@
             recv_sem=rsem.at[off], device_id={"pix": peer}, device_id_type=MESH,
         )
 
-    first = sorted({1, 2, 3, devices // 4, 3 * devices // 4, 3 * devices // 4 + 1})
+    quarter = devices // 4
+    first = sorted({1, 2, 3, quarter, quarter + 1, 2 * quarter, 2 * quarter + 1})
     later = [off for off in range(1, devices) if off not in first]
     halos = [halo_copy(off, peers[off]) for off in range(1, devices)]
     mains = {off: main_copy(off, peers[off]) for off in range(1, devices)}
@@ -219,39 +223,42 @@
             out.append(ext[2 * k + 1] + four[k + 1])
         return out
 
-    def finish(p, n):
-        for q in range(CHUNK):
-            sums = [
-                window_sums(summed[(2 * q + part) * ROWS:(2 * q + part + 1) * ROWS])
-                for part in range(2)
-            ]
-            for g in range(GROUPS):
-                real, imag = sums[0][g], sums[1][g]
-                cov[g, p, n * CHUNK + q, 0] = real
-                cov[g, p, n * CHUNK + q, 1] = real + imag
-                cov[g, p, n * CHUNK + q, 2] = imag - real
-
-    def begin(p, n):
-        one = zb[p, 0].astype(bf16), zb[p, 1].astype(bf16)
+    def finish(b, n):
+        for d in range(BATCH):
+            p = b * BATCH + d
+            for q in range(CHUNK):
+                first_row = (d * CHUNK + q) * 2 * ROWS
+                sums = [
+                    window_sums(summed[first_row + part * ROWS:first_row + (part + 1) * ROWS])
+                    for part in range(2)
+                ]
+                for g in range(GROUPS):
+                    real, imag = sums[0][g], sums[1][g]
+                    cov[g, p, n * CHUNK + q, 0] = real
+                    cov[g, p, n * CHUNK + q, 1] = real + imag
+                    cov[g, p, n * CHUNK + q, 2] = imag - real
+
+    def begin(b, n):
         half = (n * CHUNK) // PACK
-        margins = pair_products(
-            (wide[0].astype(bf16), wide[1].astype(bf16)),
-            (edge[half, 0].astype(bf16), edge[half, 1].astype(bf16)),
-        )
         planes = []
-        for q in range(CHUNK):
-            k = n * CHUNK + q
-            two = zb[k, 0].astype(bf16), zb[k, 1].astype(bf16)
-            keep = tall(mask[k - half * PACK].astype(bf16))
-            for value, margin in zip(pair_products(one, two), margins):
-                planes.append(jnp.concatenate([value, margin * keep], axis=1))
+        beside = edge[half, 0].astype(bf16), edge[half, 1].astype(bf16)
+        for d in range(BATCH):
+            p = b * BATCH + d
+            one = zb[p, 0].astype(bf16), zb[p, 1].astype(bf16)
+            margins = pair_products((wide[d, 0].astype(bf16), wide[d, 1].astype(bf16)), beside)
+            for q in range(CHUNK):
+                k = n * CHUNK + q
+                two = zb[k, 0].astype(bf16), zb[k, 1].astype(bf16)
+                keep = tall(mask[k - half * PACK].astype(bf16))
+                for value, margin in zip(pair_products(one, two), margins):
+                    planes.append(jnp.concatenate([value, margin * keep], axis=1))
         summed[...] = jnp.dot(
             jnp.concatenate(planes, axis=0), both[...], preferred_element_type=f32
         )
 
-    def covariances(p, prev):
-        for q in range(per_date):
-            off = p * per_date + q
+    def covariances(b, prev):
+        for n in range(BATCH * per_date):
+            off = b * (BATCH * per_date) + n
             source = flipped(me, turns, off)
 
             @pl.when(off != 0)
@@ -261,34 +268,38 @@
                     recv_sem=rsem.at[off], device_id={"pix": source}, device_id_type=MESH,
                 ).wait_recv()
 
-        sources = [date_at(p) * per_date + q for q in range(per_date)]
-        margin = jnp.concatenate([tall_of(win[source, height:height + HALO], LANES) for source in sources], axis=1)
-        got = lax.dot_general(
-            order[...], margin, (((1,), (1,)), ((), ())), preferred_element_type=f32
-        )
-        keep = tall(mask[lax.rem(p, PACK)])
-        half = p // PACK
-        for c in range(2):
-            part = got[c * ROWS:(c + 1) * ROWS]
-            wide[c] = part
-            edge[half, c] = edge[half, c] + part * keep
-        for q, source in enumerate(sources):
+        for d in range(BATCH):
+            p = b * BATCH + d
+            sources = [date_at(p) * per_date + q for q in range(per_date)]
+            margin = jnp.concatenate(
+                [tall_of(win[source, height:height + HALO], LANES) for source in sources], axis=1
+            )
+            got = lax.dot_general(
+                order[...], margin, (((1,), (1,)), ((), ())), preferred_element_type=f32
+            )
+            keep = tall(mask[lax.rem(p, PACK)])
+            half = p // PACK
             for c in range(2):
-                stage[c, q * local_rows:(q + 1) * local_rows] = win[
-                    source, c * local_rows:(c + 1) * local_rows
-                ].astype(f32)
-        for c in range(2):
-            for g in range(GROUPS):
-                zb[p, c, g * SUB:(g + 1) * SUB] = stage[c, pl.ds(g, SUB, stride=GROUPS), :]
+                part = got[c * ROWS:(c + 1) * ROWS]
+                wide[d, c] = part
+                edge[half, c] = edge[half, c] + part * keep
+            for q, source in enumerate(sources):
+                for c in range(2):
+                    stage[d, c, q * local_rows:(q + 1) * local_rows] = win[
+                        source, c * local_rows:(c + 1) * local_rows
+                    ].astype(f32)
+            for c in range(2):
+                for g in range(GROUPS):
+                    zb[p, c, g * SUB:(g + 1) * SUB] = stage[d, c, pl.ds(g, SUB, stride=GROUPS), :]
 
         def chunk(n, prev):
             finish(*prev)
-            begin(p, n)
-            return p, n
-
-        return lax.fori_loop(0, p // CHUNK + 1, chunk, prev)
-
-    finish(*lax.fori_loop(0, DATES, covariances, (jnp.int32(0), jnp.int32(0))))
+            begin(b, n)
+            return b, n
+
+        return lax.fori_loop(0, (b * BATCH + BATCH - 1) // CHUNK + 1, chunk, prev)
+
+    finish(*lax.fori_loop(0, DATES // BATCH, covariances, (jnp.int32(0), jnp.int32(0))))
 
     ref = flipped(my_date, date_turns, ref_ref[0])
 
@@ -392,29 +403,22 @@
     ).wait()
 
 
-def spectrum_kernel(got_ref, table_ref, comp_ref, o_ref, out_ref, got, table, comp, order, out, ins, outs):
+def spectrum_kernel(got, table, comp, o_ref, out_ref, order, out, outs):
     devices, columns = got.shape[0], got.shape[3]
     local_rows = out.shape[1]
     parts = outs.shape[0] - 1
     size = devices // parts
 
-    def copy_in(n):
-        at = pl.ds(n * size, size)
-        return pltpu.make_async_copy(got_ref.at[at], got.at[at], ins.at[n])
-
     def copy_out(n):
         at = pl.ds(n * size * columns, size * columns)
         return pltpu.make_async_copy(out.at[:, :, at], o_ref.at[:, :, at], outs.at[n])
 
-    tables = pltpu.make_async_copy(table_ref, table, ins.at[parts])
-    comps = pltpu.make_async_copy(comp_ref, comp, ins.at[parts + 1])
-    tables.start()
+    for c in range(2):
+        for g in range(GROUPS):
+            order[c, pl.ds(g, SUB, stride=GROUPS), :] = comp[c, g]
+    last = pltpu.make_async_copy(order, out_ref, outs.at[parts])
+    last.start()
     for n in range(parts):
-        copy_in(n).start()
-    comps.start()
-    tables.wait()
-    for n in range(parts):
-        copy_in(n).wait()
         for m in range(0, size, 2):
             at = n * size + m
             both = jnp.concatenate(
@@ -426,12 +430,6 @@
             for c in range(2):
                 out[c, :, at * columns:(at + 2) * columns] = value[c * local_rows:(c + 1) * local_rows]
         copy_out(n).start()
-    comps.wait()
-    for c in range(2):
-        for g in range(GROUPS):
-            order[c, pl.ds(g, SUB, stride=GROUPS), :] = comp[c, g]
-    last = pltpu.make_async_copy(order, out_ref, outs.at[parts])
-    last.start()
     for n in range(parts):
         copy_out(n).wait()
     last.wait()
@@ -444,6 +442,8 @@
     per_date = ROWS // local_rows
 
     anywhere = pl.BlockSpec(memory_space=pl.ANY)
+    hbm = pl.BlockSpec(memory_space=pltpu.HBM)
+    vmem = pl.BlockSpec(memory_space=pltpu.VMEM)
     both, pick, order = window_weights(columns), pick_weights(columns), order_weights(local_rows)
     mask = block_masks()
     table = dct_weights(local_rows)
@@ -454,21 +454,21 @@
             jax.ShapeDtypeStruct((devices, GROUPS, 2 * SUB, columns), bf16),
             jax.ShapeDtypeStruct((2, GROUPS, SUB, columns), f32),
         ),
-        in_specs=[pl.BlockSpec(memory_space=pltpu.SMEM)] + [anywhere] * 5,
+        in_specs=[pl.BlockSpec(memory_space=pltpu.SMEM)] + [hbm] * 5,
         out_specs=(anywhere, anywhere),
         scratch_shapes=[
             pltpu.VMEM((2 * local_rows, strip_columns + 2 * columns), bf16),
             pltpu.VMEM((devices, 2 * local_rows + HALO, columns), bf16),
             pltpu.VMEM((devices, HALO, LANES), bf16),
             pltpu.VMEM((DATES // PACK, 2, ROWS, LANES), f32),
-            pltpu.VMEM((2, ROWS, LANES), f32),
+            pltpu.VMEM((BATCH, 2, ROWS, LANES), f32),
             pltpu.VMEM(both.shape, bf16),
             pltpu.VMEM(pick.shape, bf16),
             pltpu.VMEM(order.shape, bf16),
             pltpu.VMEM(mask.shape, f32),
-            pltpu.VMEM((2, ROWS, columns), f32),
+            pltpu.VMEM((BATCH, 2, ROWS, columns), f32),
             pltpu.VMEM((DATES, 2, ROWS, columns), f32),
-            pltpu.VMEM((2 * CHUNK * ROWS, columns), f32),
+            pltpu.VMEM((2 * BATCH * CHUNK * ROWS, columns), f32),
             pltpu.VMEM((GROUPS, SUB, columns), f32),
             pltpu.VMEM((GROUPS, DATES, DATES, 3, SUB, columns), f32),
             pltpu.VMEM((2, DATES, 3, SUB, columns), f32),
@@ -480,10 +480,16 @@
             pltpu.SemaphoreType.DMA((1,)),
         ],
         compiler_params=pltpu.CompilerParams(
-            collective_id=0, has_side_effects=True, vmem_limit_bytes=60 * 1024 * 1024
+            collective_id=0, has_side_effects=True, vmem_limit_bytes=LINK_VMEM
         ),
         name="link",
-    )(ref_date, slcs.reshape(2 * local_rows, strip_columns), both, pick, order, mask)
+    )(
+        ref_date,
+        *(
+            pltpu.with_memory_space_constraint(value, pltpu.HBM)
+            for value in (slcs.reshape(2 * local_rows, strip_columns), both, pick, order, mask)
+        ),
+    )
 
     if per_date > 1:
         table = lax.dynamic_index_in_dim(table, lax.rem(lax.axis_index("pix"), per_date), 0, False)
@@ -496,17 +502,14 @@
             jax.ShapeDtypeStruct((2, local_rows, strip_columns), f32),
             jax.ShapeDtypeStruct((2, ROWS, columns), f32),
         ),
-        in_specs=[anywhere] * 3,
-        out_specs=(anywhere, anywhere),
+        in_specs=[vmem] * 3,
+        out_specs=(hbm, hbm),
         scratch_shapes=[
-            pltpu.VMEM((devices, GROUPS, 2 * SUB, columns), bf16),
-            pltpu.VMEM(table.shape, bf16),
-            pltpu.VMEM((2, GROUPS, SUB, columns), f32),
             pltpu.VMEM((2, ROWS, columns), f32),
             pltpu.VMEM((2, local_rows, strip_columns), f32),
-            pltpu.SemaphoreType.DMA((parts + 2,)),
             pltpu.SemaphoreType.DMA((parts + 1,)),
         ],
+        compiler_params=pltpu.CompilerParams(vmem_limit_bytes=SPECTRUM_VMEM),
         name="spectrum",
     )(phases, table, compressed)
 

time: 44.7 us -> 40.4 us (0.904)
  Pallas kernels: 43.2 us -> 39 us
    pallas_call x1, Pallas kernels: 40.9 us -> 37.7 us  [on_device(): pl.pallas_call(functools.partial(link_kernel, devices), out_shape=(jax.Sh...]
    pallas_call x1, Pallas kernels: 2.33 us -> 1.23 us  [on_device(): pl.pallas_call(spectrum_kernel, out_shape=(jax.ShapeDtypeStruct((2, local...]
where the time goes in v4:
time: 40.4 us; the launch traced here: 40.3 us
  Pallas kernels  39 us (97%)
  between operations  1.3 us (3%)
    pallas_call x1, Pallas kernels, on_device(): pl.pallas_call(functools.partial(link_kernel, devices), out_shape=(jax.Sh...  37.7 us
    pallas_call x1, Pallas kernels, on_device(): pl.pallas_call(spectrum_kernel, out_shape=(jax.ShapeDtypeStruct((2, local...  1.23 us

profile of v4, /device:TPU:0, one launch (start us, length us, event | category | flops | bytes accessed | tf_op | source)
XLA Modules:
  0.0 40.3 jit_solution(15991855970081707620)
XLA Ops:
  1.3 0.0 copy-start
  1.3 37.7 %link.1 = (bf16[16,8,16,128]{3,2,1,0:T(8,128)(2,1)S(1)}, f32[2,8,8,128]{3,2,1,0:T(8,128)S(1)}) custom-call(s32[1]{0:T(128)S(6)} %copy.9.ref_ref, bf16[128,2048]{1,0:T(8,128)(2,1)} %bitcast.1, bf16[256,128]{1,0:T(8,128)(2,1)} %constant.10.clone.both_ref, bf16[16,256]{1,0:T(8,128)(2,1)} %constant.11.clone.pick_ref, bf16[128,128]{1,0:T(8,128)(2,1)} %constant.12.clone.order_ref, ...), custom_call_target="tpu_custom_call" | custom-call | tf_op jit(solution)/shard_map/link/pallas_call | solution.py:451
  39.0 0.0 copy-done
  39.0 1.2 %spectrum.1 = (f32[2,64,2048]{2,1,0:T(8,128)}, f32[2,64,128]{2,1,0:T(8,128)}) custom-call(bf16[16,8,16,128]{3,2,1,0:T(8,128)(2,1)S(1)} %get-tuple-element.4.got, bf16[128,256]{1,0:T(8,128)(2,1)S(1)} %copy-done, f32[2,8,8,128]{3,2,1,0:T(8,128)S(1)} %get-tuple-element.5.comp), custom_call_target="tpu_custom_call" | custom-call | tf_op jit(solution)/shard_map/spectrum/pallas_call | solution.py:499
Async XLA Ops:
  1.3 37.7 %copy-start = (bf16[128,256]{1,0:T(8,128)(2,1)S(1)}, bf16[128,256]{1,0:T(8,128)(2,1)}, u32[]{:S(2)}) copy-start(bf16[128,256]{1,0:T(8,128)(2,1)} %constant.16.table) | copy-start | bytes 196612

commit v5 on v4

--- a/solution.py
+++ b/solution.py
@@ -23,6 +23,9 @@
 PACK = LANES // HALO
 CHUNK = 8
 BATCH = 2
+ORDER = (0, 1, 2, 3, 4, 5, 6, 7)
+FIRST = 10
+ROUNDS = tuple((g, 1) for g in range(GROUPS))
 SPAN = 8
 SCALE = 2.0 ** -6
 LINK_VMEM = 40 * 1024 * 1024
@@ -103,6 +106,14 @@
         else:
             a = a + delta * ((b // (1 << n)) % 2)
     return a
+
+
+def chosen(b):
+    return sum(jnp.where(b == n, value, 0) for n, value in enumerate(ORDER))
+
+
+def placed(b):
+    return sum(jnp.where(b == value, n, 0) for n, value in enumerate(ORDER))
 
 
 def link_kernel(devices, ref_ref, x_ref, both_ref, pick_ref, order_ref, mask_ref,
@@ -152,10 +163,9 @@
             recv_sem=rsem.at[off], device_id={"pix": peer}, device_id_type=MESH,
         )
 
-    quarter = devices // 4
-    first = sorted({1, 2, 3, quarter, quarter + 1, 2 * quarter, 2 * quarter + 1})
-    later = [off for off in range(1, devices) if off not in first]
-    halos = [halo_copy(off, peers[off]) for off in range(1, devices)]
+    queue = [o * BATCH * per_date + n for o in ORDER for n in range(BATCH * per_date)][1:]
+    first, later = queue[:FIRST], queue[FIRST:]
+    halos = [halo_copy(off, peers[off]) for off in queue]
     mains = {off: main_copy(off, peers[off]) for off in range(1, devices)}
 
     pl.semaphore_wait(barrier, devices - 1)
@@ -204,9 +214,6 @@
     for copy in loads[2:]:
         copy.wait()
 
-    def date_at(p):
-        return flipped(my_date, date_turns, p)
-
     def tall(value):
         return tall_of(value, ROWS)
 
@@ -237,6 +244,14 @@
                     cov[g, p, n * CHUNK + q, 0] = real
                     cov[g, p, n * CHUNK + q, 1] = real + imag
                     cov[g, p, n * CHUNK + q, 2] = imag - real
+
+    def diagonal(b, n):
+        last = jnp.where(n == (b * BATCH + BATCH - 1) // CHUNK, 1.0, 0.0)
+        for g in range(GROUPS):
+            more = load[g] * last
+            for d in range(BATCH):
+                p = b * BATCH + d
+                cov[g, p, p, 0] = cov[g, p, p, 0] + more
 
     def begin(b, n):
         half = (n * CHUNK) // PACK
@@ -257,8 +272,9 @@
         )
 
     def covariances(b, prev):
+        pick_b = chosen(b)
         for n in range(BATCH * per_date):
-            off = b * (BATCH * per_date) + n
+            off = pick_b * (BATCH * per_date) + n
             source = flipped(me, turns, off)
 
             @pl.when(off != 0)
@@ -270,7 +286,8 @@
 
         for d in range(BATCH):
             p = b * BATCH + d
-            sources = [date_at(p) * per_date + q for q in range(per_date)]
+            date = flipped(my_date, date_turns, pick_b * BATCH + d)
+            sources = [date * per_date + q for q in range(per_date)]
             margin = jnp.concatenate(
                 [tall_of(win[source, height:height + HALO], LANES) for source in sources], axis=1
             )
@@ -294,27 +311,31 @@
 
         def chunk(n, prev):
             finish(*prev)
+            diagonal(*prev)
             begin(b, n)
             return b, n
 
         return lax.fori_loop(0, (b * BATCH + BATCH - 1) // CHUNK + 1, chunk, prev)
 
-    finish(*lax.fori_loop(0, DATES // BATCH, covariances, (jnp.int32(0), jnp.int32(0))))
-
-    ref = flipped(my_date, date_turns, ref_ref[0])
-
-    def send(g):
-        for off in range(1, devices):
+    last = lax.fori_loop(0, DATES // BATCH, covariances, (jnp.int32(0), jnp.int32(0)))
+    finish(*last)
+    diagonal(*last)
+
+    ref_off = flipped(my_date, date_turns, ref_ref[0])
+    ref = placed(ref_off // BATCH) * BATCH + ref_off % BATCH
+    places = [ORDER.index(n // BATCH) * BATCH + n % BATCH for n in range(DATES)]
+
+    def send(g, size):
+        at = pl.ds(g, size)
+        for off in queue:
             pltpu.make_async_remote_copy(
-                src_ref=tile.at[g, off // per_date], dst_ref=o_ref.at[me, g],
+                src_ref=tile.at[at, places[off // per_date]], dst_ref=o_ref.at[me, at],
                 send_sem=sent.at[1], recv_sem=got_sem.at[0],
                 device_id={"pix": peers[off]}, device_id_type=MESH,
             ).start()
-        pltpu.make_async_copy(tile.at[g, 0], o_ref.at[me, g], local.at[6]).start()
+        pltpu.make_async_copy(tile.at[at, 0], o_ref.at[me, at], local.at[6]).start()
 
     def solve(g, carry):
-        for i in range(DATES):
-            cov[g, i, i, 0] = cov[g, i, i, 0] + load[g]
         for i in range(DATES):
             one, two = jnp.maximum(ref, i), jnp.minimum(ref, i)
             real = cov[g, one, two, 0]
@@ -325,12 +346,13 @@
             vec[0, i, 1] = imag
             vec[0, i, 2] = real + imag
 
-        @pl.when(g > 0)
-        def _():
-            send(g - 1)
-
-        def step(t, carry):
-            src = lax.rem(t, 2)
+        for start, size in ROUNDS[:-1]:
+            @pl.when(g == start + size)
+            def _():
+                send(start, size)
+
+        def step(t):
+            src = t % 2
             for base in range(0, DATES, SPAN):
                 acc = [[None] * 3 for _ in range(SPAN)]
                 for j in range(DATES):
@@ -361,9 +383,9 @@
                     vec[1 - src, base + q, 0] = real
                     vec[1 - src, base + q, 1] = imag
                     vec[1 - src, base + q, 2] = real + imag
-            return carry
-
-        lax.fori_loop(0, POWER_ITERS - 1, step, 0)
+
+        for t in range(POWER_ITERS - 1):
+            step(t)
         last = (POWER_ITERS - 1) % 2
         total = jnp.zeros((SUB, columns), f32)
         for k in range(DATES):
@@ -391,7 +413,7 @@
         src_ref=win.at[0:devices - 1], dst_ref=win.at[0:devices - 1], send_sem=sent.at[0],
         recv_sem=rsem.at[0], device_id={"pix": peers[1]}, device_id_type=MESH,
     ).wait_send()
-    send(GROUPS - 1)
+    send(*ROUNDS[-1])
     out = pltpu.make_async_copy(comp, comp_ref, local.at[7])
     out.start()
     pltpu.make_async_copy(tile.at[:, 0], o_ref.at[me], local.at[6]).wait()
@@ -495,7 +517,7 @@
         table = lax.dynamic_index_in_dim(table, lax.rem(lax.axis_index("pix"), per_date), 0, False)
     else:
         table = table[0]
-    parts = 2
+    parts = 4
     return pl.pallas_call(
         spectrum_kernel,
         out_shape=(

time: 40.4 us -> 39.4 us (0.975)
  Pallas kernels: 39 us -> 38 us
    pallas_call x1, Pallas kernels: 37.7 us -> 36.8 us  [on_device(): pl.pallas_call(functools.partial(link_kernel, devices), out_shape=(jax.Sh...]
where the time goes in v5:
time: 39.4 us; the launch traced here: 39.3 us
  Pallas kernels  38 us (96%)
  between operations  1.3 us (3%)
    pallas_call x1, Pallas kernels, on_device(): pl.pallas_call(functools.partial(link_kernel, devices), out_shape=(jax.Sh...  36.8 us
    pallas_call x1, Pallas kernels, on_device(): pl.pallas_call(spectrum_kernel, out_shape=(jax.ShapeDtypeStruct((2, local...  1.21 us

profile of v5, /device:TPU:0, one launch (start us, length us, event | category | flops | bytes accessed | tf_op | source)
XLA Modules:
  0.0 39.3 jit_solution(12669103326495869403)
XLA Ops:
  1.3 0.0 copy-start
  1.3 36.8 %link.1 = (bf16[16,8,16,128]{3,2,1,0:T(8,128)(2,1)S(1)}, f32[2,8,8,128]{3,2,1,0:T(8,128)S(1)}) custom-call(s32[1]{0:T(128)S(6)} %copy.9.ref_ref, bf16[128,2048]{1,0:T(8,128)(2,1)} %bitcast.1, bf16[256,128]{1,0:T(8,128)(2,1)} %constant.10.clone.both_ref, bf16[16,256]{1,0:T(8,128)(2,1)} %constant.11.clone.pick_ref, bf16[128,128]{1,0:T(8,128)(2,1)} %constant.12.clone.order_ref, ...), custom_call_target="tpu_custom_call" | custom-call | tf_op jit(solution)/shard_map/link/pallas_call | solution.py:473
  38.1 0.0 copy-done
  38.1 1.2 %spectrum.1 = (f32[2,64,2048]{2,1,0:T(8,128)}, f32[2,64,128]{2,1,0:T(8,128)}) custom-call(bf16[16,8,16,128]{3,2,1,0:T(8,128)(2,1)S(1)} %get-tuple-element.4.got, bf16[128,256]{1,0:T(8,128)(2,1)S(1)} %copy-done, f32[2,8,8,128]{3,2,1,0:T(8,128)S(1)} %get-tuple-element.5.comp), custom_call_target="tpu_custom_call" | custom-call | tf_op jit(solution)/shard_map/spectrum/pallas_call | solution.py:521
Async XLA Ops:
  1.3 36.8 %copy-start = (bf16[128,256]{1,0:T(8,128)(2,1)S(1)}, bf16[128,256]{1,0:T(8,128)(2,1)}, u32[]{:S(2)}) copy-start(bf16[128,256]{1,0:T(8,128)(2,1)} %constant.16.table) | copy-start | bytes 196612

commit v6 on v5

--- a/solution.py
+++ b/solution.py
@@ -20,12 +20,12 @@
 SUB = 8
 GROUPS = ROWS // SUB
 HALO = 16
+EDGE = 2 * HALF_X
 PACK = LANES // HALO
 CHUNK = 8
 BATCH = 2
 ORDER = (0, 1, 2, 3, 4, 5, 6, 7)
 FIRST = 10
-ROUNDS = tuple((g, 1) for g in range(GROUPS))
 SPAN = 8
 SCALE = 2.0 ** -6
 LINK_VMEM = 40 * 1024 * 1024
@@ -118,9 +118,9 @@
 
 def link_kernel(devices, ref_ref, x_ref, both_ref, pick_ref, order_ref, mask_ref,
                 o_ref, comp_ref,
-                xs, win, hsend, edge, wide, both, pick, order, mask,
+                xs, win, hsend, hwin, edge, wide, both, pick, order, mask,
                 stage, zb, summed, load, cov, vec, tile, comp,
-                local, sent, rsem, got_sem):
+                local, sent, rsem, hsem, got_sem):
     columns = win.shape[2]
     height = x_ref.shape[0]
     local_rows = height // 2
@@ -144,7 +144,7 @@
         pltpu.make_async_copy(src, dst, local.at[n])
         for n, (src, dst) in enumerate((
             (x_ref, xs.at[:, columns:columns + strip_columns]),
-            (pick_ref, pick), (block(me), win.at[me, 0:height]), (both_ref, both), (order_ref, order),
+            (pick_ref, pick), (block(me), win.at[me]), (both_ref, both), (order_ref, order),
             (mask_ref, mask),
         ))
     ]
@@ -153,14 +153,14 @@
 
     def main_copy(off, peer):
         return pltpu.make_async_remote_copy(
-            src_ref=block(peer), dst_ref=win.at[me, 0:height], send_sem=sent.at[0],
+            src_ref=block(peer), dst_ref=win.at[me], send_sem=sent.at[0],
             recv_sem=rsem.at[off], device_id={"pix": peer}, device_id_type=MESH,
         )
 
     def halo_copy(off, peer):
         return pltpu.make_async_remote_copy(
-            src_ref=hsend.at[peer], dst_ref=win.at[me, height:height + HALO], send_sem=sent.at[0],
-            recv_sem=rsem.at[off], device_id={"pix": peer}, device_id_type=MESH,
+            src_ref=hsend.at[peer], dst_ref=hwin.at[me], send_sem=sent.at[2],
+            recv_sem=hsem.at[off], device_id={"pix": peer}, device_id_type=MESH,
         )
 
     queue = [o * BATCH * per_date + n for o in ORDER for n in range(BATCH * per_date)][1:]
@@ -192,11 +192,12 @@
             got = lax.dot_general(
                 pick[...], near, (((1,), (1,)), ((), ())), preferred_element_type=f32
             )
-            hsend[n * blocks + q] = got.astype(bf16)
+            for r in range(EDGE // 2):
+                hsend[n * blocks + q, r] = got[2 * r:2 * r + 2].astype(bf16)
         return carry
 
     lax.fori_loop(0, devices // blocks, cut_halos, 0)
-    win[me, height:height + HALO] = hsend[me]
+    hwin[me] = hsend[me]
     for c in halos:
         c.start()
     for off in later:
@@ -271,6 +272,10 @@
             jnp.concatenate(planes, axis=0), both[...], preferred_element_type=f32
         )
 
+    def rows_of(ref, source):
+        rows = [ref[source, r].astype(f32) for r in range(EDGE // 2)]
+        return jnp.concatenate(rows + [jnp.zeros((HALO - EDGE, LANES), f32)], axis=0).astype(bf16)
+
     def covariances(b, prev):
         pick_b = chosen(b)
         for n in range(BATCH * per_date):
@@ -280,6 +285,10 @@
             @pl.when(off != 0)
             def _():
                 pltpu.make_async_remote_copy(
+                    src_ref=hwin.at[source], dst_ref=hwin.at[source], send_sem=sent.at[2],
+                    recv_sem=hsem.at[off], device_id={"pix": source}, device_id_type=MESH,
+                ).wait_recv()
+                pltpu.make_async_remote_copy(
                     src_ref=win.at[source], dst_ref=win.at[source], send_sem=sent.at[0],
                     recv_sem=rsem.at[off], device_id={"pix": source}, device_id_type=MESH,
                 ).wait_recv()
@@ -289,7 +298,7 @@
             date = flipped(my_date, date_turns, pick_b * BATCH + d)
             sources = [date * per_date + q for q in range(per_date)]
             margin = jnp.concatenate(
-                [tall_of(win[source, height:height + HALO], LANES) for source in sources], axis=1
+                [tall_of(rows_of(hwin, source), LANES) for source in sources], axis=1
             )
             got = lax.dot_general(
                 order[...], margin, (((1,), (1,)), ((), ())), preferred_element_type=f32
@@ -325,15 +334,14 @@
     ref = placed(ref_off // BATCH) * BATCH + ref_off % BATCH
     places = [ORDER.index(n // BATCH) * BATCH + n % BATCH for n in range(DATES)]
 
-    def send(g, size):
-        at = pl.ds(g, size)
+    def send(g):
         for off in queue:
             pltpu.make_async_remote_copy(
-                src_ref=tile.at[at, places[off // per_date]], dst_ref=o_ref.at[me, at],
+                src_ref=tile.at[g, places[off // per_date]], dst_ref=o_ref.at[me, g],
                 send_sem=sent.at[1], recv_sem=got_sem.at[0],
                 device_id={"pix": peers[off]}, device_id_type=MESH,
             ).start()
-        pltpu.make_async_copy(tile.at[at, 0], o_ref.at[me, at], local.at[6]).start()
+        pltpu.make_async_copy(tile.at[g, 0], o_ref.at[me, g], local.at[6]).start()
 
     def solve(g, carry):
         for i in range(DATES):
@@ -346,10 +354,9 @@
             vec[0, i, 1] = imag
             vec[0, i, 2] = real + imag
 
-        for start, size in ROUNDS[:-1]:
-            @pl.when(g == start + size)
-            def _():
-                send(start, size)
+        @pl.when(g > 0)
+        def _():
+            send(g - 1)
 
         def step(t):
             src = t % 2
@@ -413,7 +420,11 @@
         src_ref=win.at[0:devices - 1], dst_ref=win.at[0:devices - 1], send_sem=sent.at[0],
         recv_sem=rsem.at[0], device_id={"pix": peers[1]}, device_id_type=MESH,
     ).wait_send()
-    send(*ROUNDS[-1])
+    pltpu.make_async_remote_copy(
+        src_ref=hwin.at[0:devices - 1], dst_ref=hwin.at[0:devices - 1], send_sem=sent.at[2],
+        recv_sem=hsem.at[0], device_id={"pix": peers[1]}, device_id_type=MESH,
+    ).wait_send()
+    send(GROUPS - 1)
     out = pltpu.make_async_copy(comp, comp_ref, local.at[7])
     out.start()
     pltpu.make_async_copy(tile.at[:, 0], o_ref.at[me], local.at[6]).wait()
@@ -480,8 +491,9 @@
         out_specs=(anywhere, anywhere),
         scratch_shapes=[
             pltpu.VMEM((2 * local_rows, strip_columns + 2 * columns), bf16),
-            pltpu.VMEM((devices, 2 * local_rows + HALO, columns), bf16),
-            pltpu.VMEM((devices, HALO, LANES), bf16),
+            pltpu.VMEM((devices, 2 * local_rows, columns), bf16),
+            pltpu.VMEM((devices, EDGE // 2, 2, LANES), bf16),
+            pltpu.VMEM((devices, EDGE // 2, 2, LANES), bf16),
             pltpu.VMEM((DATES // PACK, 2, ROWS, LANES), f32),
             pltpu.VMEM((BATCH, 2, ROWS, LANES), f32),
             pltpu.VMEM(both.shape, bf16),
@@ -497,7 +509,8 @@
             pltpu.VMEM((GROUPS, DATES, 2 * SUB, columns), bf16),
             pltpu.VMEM((2, GROUPS, SUB, columns), f32),
             pltpu.SemaphoreType.DMA((8,)),
-            pltpu.SemaphoreType.DMA((2,)),
+            pltpu.SemaphoreType.DMA((3,)),
+            pltpu.SemaphoreType.DMA((devices,)),
             pltpu.SemaphoreType.DMA((devices,)),
             pltpu.SemaphoreType.DMA((1,)),
         ],

time: 39.4 us -> 39.1 us (level)
  Pallas kernels: 38 us -> 37.6 us
where the time goes in v6:
time: 39.1 us; the launch traced here: 38.9 us
  Pallas kernels  37.6 us (96%)
  between operations  1.3 us (3%)
    pallas_call x1, Pallas kernels, on_device(): pl.pallas_call(functools.partial(link_kernel, devices), out_shape=(jax.Sh...  36.4 us
    pallas_call x1, Pallas kernels, on_device(): pl.pallas_call(spectrum_kernel, out_shape=(jax.ShapeDtypeStruct((2, local...  1.21 us

profile of v6, /device:TPU:0, one launch (start us, length us, event | category | flops | bytes accessed | tf_op | source)
XLA Modules:
  0.0 38.9 jit_solution(14191875503433364680)
XLA Ops:
  1.3 0.0 copy-start
  1.3 36.4 %link.1 = (bf16[16,8,16,128]{3,2,1,0:T(8,128)(2,1)S(1)}, f32[2,8,8,128]{3,2,1,0:T(8,128)S(1)}) custom-call(s32[1]{0:T(128)S(6)} %copy.9.ref_ref, bf16[128,2048]{1,0:T(8,128)(2,1)} %bitcast.1, bf16[256,128]{1,0:T(8,128)(2,1)} %constant.10.clone.both_ref, bf16[16,256]{1,0:T(8,128)(2,1)} %constant.11.clone.pick_ref, bf16[128,128]{1,0:T(8,128)(2,1)} %constant.12.clone.order_ref, ...), custom_call_target="tpu_custom_call" | custom-call | tf_op jit(solution)/shard_map/link/pallas_call | solution.py:484
  37.7 0.0 copy-done
  37.7 1.2 %spectrum.1 = (f32[2,64,2048]{2,1,0:T(8,128)}, f32[2,64,128]{2,1,0:T(8,128)}) custom-call(bf16[16,8,16,128]{3,2,1,0:T(8,128)(2,1)S(1)} %get-tuple-element.4.got, bf16[128,256]{1,0:T(8,128)(2,1)S(1)} %copy-done, f32[2,8,8,128]{3,2,1,0:T(8,128)S(1)} %get-tuple-element.5.comp), custom_call_target="tpu_custom_call" | custom-call | tf_op jit(solution)/shard_map/spectrum/pallas_call | solution.py:534
Async XLA Ops:
  1.3 36.4 %copy-start = (bf16[128,256]{1,0:T(8,128)(2,1)S(1)}, bf16[128,256]{1,0:T(8,128)(2,1)}, u32[]{:S(2)}) copy-start(bf16[128,256]{1,0:T(8,128)(2,1)} %constant.16.table) | copy-start | bytes 196612

commit v7 on v6

--- a/solution.py
+++ b/solution.py
@@ -24,7 +24,6 @@
 PACK = LANES // HALO
 CHUNK = 8
 BATCH = 2
-ORDER = (0, 1, 2, 3, 4, 5, 6, 7)
 FIRST = 10
 SPAN = 8
 SCALE = 2.0 ** -6
@@ -106,14 +105,6 @@
         else:
             a = a + delta * ((b // (1 << n)) % 2)
     return a
-
-
-def chosen(b):
-    return sum(jnp.where(b == n, value, 0) for n, value in enumerate(ORDER))
-
-
-def placed(b):
-    return sum(jnp.where(b == value, n, 0) for n, value in enumerate(ORDER))
 
 
 def link_kernel(devices, ref_ref, x_ref, both_ref, pick_ref, order_ref, mask_ref,
@@ -163,7 +154,7 @@
             recv_sem=hsem.at[off], device_id={"pix": peer}, device_id_type=MESH,
         )
 
-    queue = [o * BATCH * per_date + n for o in ORDER for n in range(BATCH * per_date)][1:]
+    queue = list(range(1, devices))
     first, later = queue[:FIRST], queue[FIRST:]
     halos = [halo_copy(off, peers[off]) for off in queue]
     mains = {off: main_copy(off, peers[off]) for off in range(1, devices)}
@@ -277,9 +268,8 @@
         return jnp.concatenate(rows + [jnp.zeros((HALO - EDGE, LANES), f32)], axis=0).astype(bf16)
 
     def covariances(b, prev):
-        pick_b = chosen(b)
         for n in range(BATCH * per_date):
-            off = pick_b * (BATCH * per_date) + n
+            off = b * (BATCH * per_date) + n
             source = flipped(me, turns, off)
 
             @pl.when(off != 0)
@@ -295,7 +285,7 @@
 
         for d in range(BATCH):
             p = b * BATCH + d
-            date = flipped(my_date, date_turns, pick_b * BATCH + d)
+            date = flipped(my_date, date_turns, p)
             sources = [date * per_date + q for q in range(per_date)]
             margin = jnp.concatenate(
                 [tall_of(rows_of(hwin, source), LANES) for source in sources], axis=1
@@ -330,26 +320,29 @@
     finish(*last)
     diagonal(*last)
 
-    ref_off = flipped(my_date, date_turns, ref_ref[0])
-    ref = placed(ref_off // BATCH) * BATCH + ref_off % BATCH
-    places = [ORDER.index(n // BATCH) * BATCH + n % BATCH for n in range(DATES)]
+    ref = flipped(my_date, date_turns, ref_ref[0])
 
     def send(g):
         for off in queue:
             pltpu.make_async_remote_copy(
-                src_ref=tile.at[g, places[off // per_date]], dst_ref=o_ref.at[me, g],
+                src_ref=tile.at[g, off // per_date], dst_ref=o_ref.at[me, g],
                 send_sem=sent.at[1], recv_sem=got_sem.at[0],
                 device_id={"pix": peers[off]}, device_id_type=MESH,
             ).start()
         pltpu.make_async_copy(tile.at[g, 0], o_ref.at[me, g], local.at[6]).start()
 
+    column = [
+        (
+            jnp.maximum(ref, i), jnp.minimum(ref, i),
+            jnp.where(ref == i, 0.0, jnp.where(ref < i, 0.5, -0.5)),
+        )
+        for i in range(DATES)
+    ]
+
     def solve(g, carry):
-        for i in range(DATES):
-            one, two = jnp.maximum(ref, i), jnp.minimum(ref, i)
+        for i, (one, two, sign) in enumerate(column):
             real = cov[g, one, two, 0]
-            imag = 0.5 * (cov[g, one, two, 1] + cov[g, one, two, 2])
-            sign = jnp.where(ref == i, 0.0, jnp.where(ref < i, 1.0, -1.0))
-            imag = imag * sign
+            imag = (cov[g, one, two, 1] + cov[g, one, two, 2]) * sign
             vec[0, i, 0] = real
             vec[0, i, 1] = imag
             vec[0, i, 2] = real + imag

time: 39.1 us -> 39 us (level)
  no operation moved by 1% of the time
where the time goes in v7:
time: 39 us; the launch traced here: 38.8 us
  Pallas kernels  37.5 us (96%)
  between operations  1.3 us (3%)
    pallas_call x1, Pallas kernels, on_device(): pl.pallas_call(functools.partial(link_kernel, devices), out_shape=(jax.Sh...  36.3 us
    pallas_call x1, Pallas kernels, on_device(): pl.pallas_call(spectrum_kernel, out_shape=(jax.ShapeDtypeStruct((2, local...  1.21 us

profile of v7, /device:TPU:0, one launch (start us, length us, event | category | flops | bytes accessed | tf_op | source)
XLA Modules:
  0.0 38.8 jit_solution(5844526361423769743)
XLA Ops:
  1.3 0.0 copy-start
  1.3 36.3 %link.1 = (bf16[16,8,16,128]{3,2,1,0:T(8,128)(2,1)S(1)}, f32[2,8,8,128]{3,2,1,0:T(8,128)S(1)}) custom-call(s32[1]{0:T(128)S(6)} %copy.9.ref_ref, bf16[128,2048]{1,0:T(8,128)(2,1)} %bitcast.1, bf16[256,128]{1,0:T(8,128)(2,1)} %constant.10.clone.both_ref, bf16[16,256]{1,0:T(8,128)(2,1)} %constant.11.clone.pick_ref, bf16[128,128]{1,0:T(8,128)(2,1)} %constant.12.clone.order_ref, ...), custom_call_target="tpu_custom_call" | custom-call | tf_op jit(solution)/shard_map/link/pallas_call | solution.py:477
  37.6 0.0 copy-done
  37.6 1.2 %spectrum.1 = (f32[2,64,2048]{2,1,0:T(8,128)}, f32[2,64,128]{2,1,0:T(8,128)}) custom-call(bf16[16,8,16,128]{3,2,1,0:T(8,128)(2,1)S(1)} %get-tuple-element.4.got, bf16[128,256]{1,0:T(8,128)(2,1)S(1)} %copy-done, f32[2,8,8,128]{3,2,1,0:T(8,128)S(1)} %get-tuple-element.5.comp), custom_call_target="tpu_custom_call" | custom-call | tf_op jit(solution)/shard_map/spectrum/pallas_call | solution.py:527
Async XLA Ops:
  1.3 36.3 %copy-start = (bf16[128,256]{1,0:T(8,128)(2,1)S(1)}, bf16[128,256]{1,0:T(8,128)(2,1)}, u32[]{:S(2)}) copy-start(bf16[128,256]{1,0:T(8,128)(2,1)} %constant.16.table) | copy-start | bytes 196612

commit v8 on v7

--- a/solution.py
+++ b/solution.py
@@ -24,7 +24,7 @@
 PACK = LANES // HALO
 CHUNK = 8
 BATCH = 2
-FIRST = 10
+FIRST = 8
 SPAN = 8
 SCALE = 2.0 ** -6
 LINK_VMEM = 40 * 1024 * 1024
@@ -110,7 +110,7 @@
 def link_kernel(devices, ref_ref, x_ref, both_ref, pick_ref, order_ref, mask_ref,
                 o_ref, comp_ref,
                 xs, win, hsend, hwin, edge, wide, both, pick, order, mask,
-                stage, zb, summed, load, cov, vec, tile, comp,
+                stage, zb, summed, spare, load, cov, vec, tile, comp,
                 local, sent, rsem, hsem, got_sem):
     columns = win.shape[2]
     height = x_ref.shape[0]
@@ -222,13 +222,13 @@
             out.append(ext[2 * k + 1] + four[k + 1])
         return out
 
-    def finish(b, n):
+    def finish(held, b, n):
         for d in range(BATCH):
             p = b * BATCH + d
             for q in range(CHUNK):
                 first_row = (d * CHUNK + q) * 2 * ROWS
                 sums = [
-                    window_sums(summed[first_row + part * ROWS:first_row + (part + 1) * ROWS])
+                    window_sums(held[first_row + part * ROWS:first_row + (part + 1) * ROWS])
                     for part in range(2)
                 ]
                 for g in range(GROUPS):
@@ -237,15 +237,14 @@
                     cov[g, p, n * CHUNK + q, 1] = real + imag
                     cov[g, p, n * CHUNK + q, 2] = imag - real
 
-    def diagonal(b, n):
-        last = jnp.where(n == (b * BATCH + BATCH - 1) // CHUNK, 1.0, 0.0)
+    def diagonal(b):
         for g in range(GROUPS):
-            more = load[g] * last
+            more = load[g]
             for d in range(BATCH):
                 p = b * BATCH + d
                 cov[g, p, p, 0] = cov[g, p, p, 0] + more
 
-    def begin(b, n):
+    def begin(held, b, n):
         half = (n * CHUNK) // PACK
         planes = []
         beside = edge[half, 0].astype(bf16), edge[half, 1].astype(bf16)
@@ -259,7 +258,7 @@
                 keep = tall(mask[k - half * PACK].astype(bf16))
                 for value, margin in zip(pair_products(one, two), margins):
                     planes.append(jnp.concatenate([value, margin * keep], axis=1))
-        summed[...] = jnp.dot(
+        held[...] = jnp.dot(
             jnp.concatenate(planes, axis=0), both[...], preferred_element_type=f32
         )
 
@@ -267,7 +266,7 @@
         rows = [ref[source, r].astype(f32) for r in range(EDGE // 2)]
         return jnp.concatenate(rows + [jnp.zeros((HALO - EDGE, LANES), f32)], axis=0).astype(bf16)
 
-    def covariances(b, prev):
+    def covariances(chunks, b, prev):
         for n in range(BATCH * per_date):
             off = b * (BATCH * per_date) + n
             source = flipped(me, turns, off)
@@ -308,17 +307,20 @@
                 for g in range(GROUPS):
                     zb[p, c, g * SUB:(g + 1) * SUB] = stage[d, c, pl.ds(g, SUB, stride=GROUPS), :]
 
-        def chunk(n, prev):
-            finish(*prev)
-            diagonal(*prev)
-            begin(b, n)
-            return b, n
-
-        return lax.fori_loop(0, (b * BATCH + BATCH - 1) // CHUNK + 1, chunk, prev)
-
-    last = lax.fori_loop(0, DATES // BATCH, covariances, (jnp.int32(0), jnp.int32(0)))
-    finish(*last)
-    diagonal(*last)
+        for n in range(chunks - 1):
+            begin(spare, b, n)
+        finish(summed, prev, prev * BATCH // CHUNK)
+        diagonal(prev)
+        begin(summed, b, chunks - 1)
+        for n in range(chunks - 1):
+            finish(spare, b, n)
+        return b
+
+    middle = CHUNK // BATCH
+    last = lax.fori_loop(0, middle, functools.partial(covariances, 1), jnp.int32(0))
+    last = lax.fori_loop(middle, 2 * middle, functools.partial(covariances, 2), last)
+    finish(summed, last, 1)
+    diagonal(last)
 
     ref = flipped(my_date, date_turns, ref_ref[0])
 
@@ -496,6 +498,7 @@
             pltpu.VMEM((BATCH, 2, ROWS, columns), f32),
             pltpu.VMEM((DATES, 2, ROWS, columns), f32),
             pltpu.VMEM((2 * BATCH * CHUNK * ROWS, columns), f32),
+            pltpu.VMEM((2 * BATCH * CHUNK * ROWS, columns), f32),
             pltpu.VMEM((GROUPS, SUB, columns), f32),
             pltpu.VMEM((GROUPS, DATES, DATES, 3, SUB, columns), f32),
             pltpu.VMEM((2, DATES, 3, SUB, columns), f32),

time: 39 us -> 38.8 us (level)
  no operation moved by 1% of the time
where the time goes in v8:
time: 38.8 us; the launch traced here: 38.7 us
  Pallas kernels  37.4 us (96%)
  between operations  1.3 us (3%)
    pallas_call x1, Pallas kernels, on_device(): pl.pallas_call(functools.partial(link_kernel, devices), out_shape=(jax.Sh...  36.1 us
    pallas_call x1, Pallas kernels, on_device(): pl.pallas_call(spectrum_kernel, out_shape=(jax.ShapeDtypeStruct((2, local...  1.21 us

profile of v8, /device:TPU:0, one launch (start us, length us, event | category | flops | bytes accessed | tf_op | source)
XLA Modules:
  0.0 38.7 jit_solution(7454416581945175963)
XLA Ops:
  1.3 0.0 copy-start
  1.3 36.1 %link.1 = (bf16[16,8,16,128]{3,2,1,0:T(8,128)(2,1)S(1)}, f32[2,8,8,128]{3,2,1,0:T(8,128)S(1)}) custom-call(s32[1]{0:T(128)S(6)} %copy.9.ref_ref, bf16[128,2048]{1,0:T(8,128)(2,1)} %bitcast.1, bf16[256,128]{1,0:T(8,128)(2,1)} %constant.10.clone.both_ref, bf16[16,256]{1,0:T(8,128)(2,1)} %constant.11.clone.pick_ref, bf16[128,128]{1,0:T(8,128)(2,1)} %constant.12.clone.order_ref, ...), custom_call_target="tpu_custom_call" | custom-call | tf_op jit(solution)/shard_map/link/pallas_call | solution.py:479
  37.4 0.0 copy-done
  37.4 1.2 %spectrum.1 = (f32[2,64,2048]{2,1,0:T(8,128)}, f32[2,64,128]{2,1,0:T(8,128)}) custom-call(bf16[16,8,16,128]{3,2,1,0:T(8,128)(2,1)S(1)} %get-tuple-element.4.got, bf16[128,256]{1,0:T(8,128)(2,1)S(1)} %copy-done, f32[2,8,8,128]{3,2,1,0:T(8,128)S(1)} %get-tuple-element.5.comp), custom_call_target="tpu_custom_call" | custom-call | tf_op jit(solution)/shard_map/spectrum/pallas_call | solution.py:530
Async XLA Ops:
  1.3 36.2 %copy-start = (bf16[128,256]{1,0:T(8,128)(2,1)S(1)}, bf16[128,256]{1,0:T(8,128)(2,1)}, u32[]{:S(2)}) copy-start(bf16[128,256]{1,0:T(8,128)(2,1)} %constant.16.table) | copy-start | bytes 196612
